TPU v7x, 8 devices: a whole 2x2x1 slice. The times are simulated.
8 devices in a mesh: dp: 1 (over z), sp: 8 (over y, x, core).
Axes of the slice: x: 2, y: 2, z: 1, core: 2. Of those that a mesh axis runs over, the one named last changes fastest.
Arguments:
- x_one: bfloat16 [512, 1792], P(('dp', 'sp'))
- seg_one: int32 [512], P(('dp', 'sp'))
- pos_one: int32 [512], P(('dp', 'sp'))
- x_two: bfloat16 [512, 1792], P(('dp', 'sp'))
- seg_two: int32 [512], P(('dp', 'sp'))
- pos_two: int32 [512], P(('dp', 'sp'))
- w_qdown: bfloat16 [1792, 384], replicated
- gain_q: bfloat16 [384], replicated
- w_qup: bfloat16 [384, 6144], replicated
- w_kvdown: bfloat16 [1792, 576], replicated
- gain_kv: bfloat16 [512], replicated
- w_kvup: bfloat16 [512, 8192], replicated
- w_out: bfloat16 [4096, 1792], replicated
Outputs:
- output 1: bfloat16 [512, 1792], P(('dp', 'sp'))
- output 2: bfloat16 [512, 1792], P(('dp', 'sp'))
All inputs are finite; a program needn't handle non-finite values.
Results may differ from a plain program's by a relative error of at most 0.0139461.
Values are sent between devices in bfloat16 or wider.
A program may use at most 1 GiB of HBM per device.

v0:
```python
import jax
import jax.numpy as jnp
from jax import lax
from jax.experimental import pallas as pl
from jax.experimental.pallas import tpu as pltpu
from jax.sharding import PartitionSpec as P

MESH = pl.DeviceIdType.MESH
F32 = jnp.float32
BF16 = jnp.bfloat16

D_MODEL = 1792
Q_LAT = 384
KV_LAT = 512
ROPE = 64
NOPE = 128
HEADS = 16
BLK = 64
CHIP = 2 * BLK
TOK = 512
NCHIP = 4
LN_BASE = 9.210340371976184
EPS = 1e-6
SCALE2 = 192 ** -0.5 * 1.4426950408889634
NEG = -1e30
BIG = 3.0e38


def norm_rows(z, gain):
    ms = jnp.mean(z * z, axis=-1, keepdims=True)
    return (z * lax.rsqrt(ms + EPS) * gain.astype(F32)[None, :]).astype(BF16)


def body(x1, p1, x2, p2, wqd, gq, wqu, wkvd, gkv, wkvu, wo, y,
         xv, posv, wqd_v, gq_v, wqu_v, wkvd_v, gkv_v, wkvu_v, wo_v,
         kvlat, ropeb, qlat, tabs, qbuf, kvb, bias, oall, oin,
         lsem, ds, dr, fs, fr, qs, qr, os_, or_):
    sp = lax.axis_index("sp")
    dp = lax.axis_index("dp")
    k = lax.rem(sp, 2)
    c = lax.div(sp, 2)
    pk = 1 - k

    def dev(chip, core):
        return (dp, chip * 2 + core)

    partner = dev(c, pk)

    def local(src, dst, i):
        cp = pltpu.make_async_copy(src, dst, lsem.at[i])
        cp.start()
        return cp

    l_x1 = local(x1, xv.at[pl.ds(0, BLK)], 0)
    l_x2 = local(x2, xv.at[pl.ds(BLK, BLK)], 1)
    l_p1 = local(p1, posv.at[0], 2)
    l_p2 = local(p2, posv.at[1], 3)
    l_gkv = local(gkv, gkv_v, 4)
    l_wkvd = local(wkvd, wkvd_v, 5)
    l_gq = local(gq, gq_v, 6)
    l_wqd = local(wqd, wqd_v, 7)
    l_wkvu = [local(wkvu.at[:, pl.ds(pl.multiple_of(k * 4096 + i * 1024, 1024), 1024)], wkvu_v.at[i], 8 + i) for i in range(4)]
    l_wqu = [local(wqu.at[:, pl.ds(pl.multiple_of(k * 3072 + i * 768, 256), 768)], wqu_v.at[i], 12 + i) for i in range(4)]
    l_wo = [local(wo.at[pl.ds(i * 1024, 1024)], wo_v.at[pl.ds(i * 1024, 1024)], 16 + i) for i in range(4)]

    barrier = pltpu.get_barrier_semaphore()
    pl.semaphore_signal(barrier, inc=1, device_id=partner, device_id_type=MESH)
    for j in range(1, NCHIP):
        pl.semaphore_signal(barrier, inc=1, device_id=dev(lax.rem(c + j, NCHIP), k), device_id_type=MESH)

    for b in range(1, NCHIP):
        @pl.when(c < b)
        def _():
            ropeb[pl.ds(b * CHIP, CHIP)] = jnp.zeros((CHIP, 128), BF16)

            def zero(h, _):
                for mb in range(2):
                    kvb[mb, h, pl.ds(b * CHIP, CHIP)] = jnp.zeros((CHIP, 256), BF16)
                return 0
            lax.fori_loop(0, HEADS, zero, 0)

    lane = lax.broadcasted_iota(jnp.int32, (1, 128), 1)
    lo64 = lane < 64
    lo32 = lax.rem(lane, 64) < 32

    l_p1.wait()
    l_p2.wait()
    own = pl.ds(pl.multiple_of(k * CHIP, CHIP), CHIP)
    eye = lax.broadcasted_iota(jnp.int32, (BLK, BLK), 0) == lax.broadcasted_iota(jnp.int32, (BLK, BLK), 1)
    cols = [jnp.sum(jnp.where(eye, posv[mb].astype(F32), 0.0), axis=1, keepdims=True) for mb in range(2)]
    pos_col = jnp.concatenate(cols, axis=0)
    freq = jnp.exp(lax.rem(lane, 32).astype(F32) * (-LN_BASE / 32))
    ang = pos_col * freq
    cos_t = jnp.cos(ang)
    sin_t = jnp.sin(ang)
    sin_t = jnp.where(lo32, -sin_t, sin_t)
    tabs[0, own] = cos_t
    tabs[1, own] = sin_t
    tabs[2, own] = pos_col + jnp.zeros((CHIP, 128), F32)

    def rot(z, cs, sn):
        sw = jnp.where(lo32, pltpu.roll(z, 96, 1), pltpu.roll(z, 32, 1))
        return z * cs + sw * sn

    with jax.named_scope("wait_x"):
        l_x1.wait()
        l_x2.wait()
        l_gkv.wait()
        l_wkvd.wait()
    u = lax.dot_general(xv[...], wkvd_v[...], (((1,), (1,)), ((), ())), preferred_element_type=F32)
    ckv = norm_rows(u[:, :KV_LAT], gkv_v[...])
    ur = u[:, KV_LAT:]
    kr = rot(jnp.concatenate([ur, ur], axis=1), cos_t, sin_t)
    kr = jnp.where(lo64, kr[:BLK], kr[BLK:]).astype(BF16)

    def rows(chip, core):
        return pl.ds(pl.multiple_of(chip * CHIP + core * BLK, BLK), BLK)

    def part(item, chip, core):
        r = rows(chip, core)
        return ropeb.at[r] if item == 0 else kvlat.at[item - 1, r]

    ropeb[rows(c, k)] = kr
    kvlat[0, rows(c, k)] = ckv[:BLK]
    kvlat[1, rows(c, k)] = ckv[BLK:]

    with jax.named_scope("barrier"):
        pl.semaphore_wait(barrier, 4)

    def direct(item, j):
        p = part(item, c, k)
        return pltpu.make_async_remote_copy(src_ref=p, dst_ref=p, send_sem=ds.at[item, j - 1], recv_sem=dr.at[item, c],
                                            device_id=dev(c + j, k), device_id_type=MESH)

    def direct_recv(item, chip):
        p = part(item, chip, k)
        return pltpu.make_async_remote_copy(src_ref=p, dst_ref=p, send_sem=ds.at[item, 0], recv_sem=dr.at[item, chip],
                                            device_id=partner, device_id_type=MESH)

    def forward(item, chip):
        p = part(item, chip, k)
        return pltpu.make_async_remote_copy(src_ref=p, dst_ref=p, send_sem=fs.at[item, chip], recv_sem=fr.at[item, chip],
                                            device_id=partner, device_id_type=MESH)

    def forward_recv(item, chip):
        p = part(item, chip, pk)
        return pltpu.make_async_remote_copy(src_ref=p, dst_ref=p, send_sem=fs.at[item, chip], recv_sem=fr.at[item, chip],
                                            device_id=partner, device_id_type=MESH)

    for item in range(3):
        for j in (3, 2, 1):
            @pl.when(c + j < NCHIP)
            def _():
                direct(item, j).start()
        forward(item, c).start()

    l_gq.wait()
    l_wqd.wait()
    with jax.named_scope("q_down"):
        qlat[own] = norm_rows(jnp.dot(xv[...], wqd_v[...], preferred_element_type=F32), gq_v[...])

    def q_copy(i, core):
        r = pl.ds(pl.multiple_of(core * CHIP, CHIP), CHIP)
        p = qlat.at[r] if i == 0 else tabs.at[:, r]
        return pltpu.make_async_remote_copy(src_ref=p, dst_ref=p, send_sem=qs.at[i], recv_sem=qr.at[i],
                                            device_id=partner, device_id_type=MESH)

    for i in range(2):
        q_copy(i, k).start()

    def kv_up(lhs, store):
        for i in range(4):
            kv = jnp.dot(lhs, wkvu_v[i], preferred_element_type=F32).astype(BF16)
            for h in range(4):
                store(i * 4 + h, kv[:, h * 256:(h + 1) * 256])

    def kv_up_device(core):
        r = rows(c, core)

        def store(h, val):
            kvb[0, h, r] = val[:BLK]
            kvb[1, h, r] = val[BLK:]
        kv_up(jnp.concatenate([kvlat[0, r], kvlat[1, r]], axis=0), store)

    def kv_up_chip(mb, chip):
        r = pl.ds(pl.multiple_of(chip * CHIP, CHIP), CHIP)

        def store(h, val):
            kvb[mb, h, r] = val
        kv_up(kvlat[mb, r], store)

    with jax.named_scope("wait_wkvu"):
        for cp in l_wkvu:
            cp.wait()
    with jax.named_scope("kv_own"):
        kv_up_device(k)
    for item in range(3):
        forward_recv(item, c).wait_recv()
    with jax.named_scope("kv_partner"):
        kv_up_device(pk)

    for i in range(2):
        q_copy(i, pk).wait_recv()
    for mb in range(2):
        for core in range(2):
            pos = tabs[2, pl.ds(core * CHIP + mb * BLK, BLK), 0:1].astype(jnp.int32)
            qi = c * CHIP + core * BLK + lax.broadcasted_iota(jnp.int32, (BLK, TOK), 0)
            ki = lax.broadcasted_iota(jnp.int32, (BLK, TOK), 1)
            keep = jnp.logical_and(ki <= qi, ki >= qi - pos)
            bias[mb, pl.ds(core * BLK, BLK)] = jnp.where(keep, BIG, NEG)
    for cp in l_wqu:
        cp.wait()

    def q_up(i, _):
        f = jnp.dot(qlat[...], wqu_v[i], preferred_element_type=F32)
        cs = tabs[0]
        sn = tabs[1]
        for pair in range(2):
            t0, t1, t2 = (f[:, pair * 384 + n * 128: pair * 384 + (n + 1) * 128] for n in range(3))
            n1 = pltpu.roll(jnp.where(lo64, t2, t1), 64, 1)
            r = rot(jnp.where(lo64, t1, t2), cs, sn)
            rw = pltpu.roll(r, 64, 1)
            nopes = (t0.astype(BF16), n1.astype(BF16))
            zero = jnp.zeros_like(r)
            ropes = ((jnp.where(lo64, r, zero).astype(BF16), jnp.where(lo64, rw, zero).astype(BF16)),
                     (jnp.where(lo64, zero, rw).astype(BF16), jnp.where(lo64, zero, r).astype(BF16)))
            for odd in range(2):
                h = i * 4 + pair * 2 + odd
                for mb in range(2):
                    for core in range(2):
                        s = slice(core * CHIP + mb * BLK, core * CHIP + (mb + 1) * BLK)
                        qbuf[mb, h, pl.ds(core * BLK, BLK), 0:128] = nopes[odd][s]
                        qbuf[mb, h, pl.ds(core * BLK, BLK), 128:256] = ropes[mb][odd][s]
        return 0
    with jax.named_scope("q_up"):
        lax.fori_loop(0, 4, q_up, 0)

    def pass_on(items):
        def step(j, _):
            for item in items:
                direct_recv(item, c - j).wait_recv()
                forward(item, c - j).start()
            return 0
        lax.fori_loop(1, c + 1, step, 0)

    def take(mb, items):
        def step(j, _):
            for item in items:
                forward_recv(item, c - j).wait_recv()
            kv_up_chip(mb, c - j)
            return 0
        lax.fori_loop(1, c + 1, step, 0)

    def head(mb, h):
        kv = kvb[mb, h]
        kcat = jnp.concatenate([kv[:, :NOPE], ropeb[...]], axis=1)
        s = lax.dot_general(qbuf[mb, h], kcat, (((1,), (1,)), ((), ())), preferred_element_type=F32)
        s = jnp.minimum(s, bias[mb])
        m = jnp.max(s, axis=1, keepdims=True)
        e = jnp.exp2((s - m) * SCALE2)
        p = (e * (1.0 / jnp.sum(e, axis=1, keepdims=True))).astype(BF16)
        return jnp.dot(p, kv[:, NOPE:], preferred_element_type=F32).astype(BF16)

    def heads(mb, lo, hi):
        def step(i, _):
            for u_ in range(2):
                h = i * 2 + u_
                oall[mb, :, pl.ds(pl.multiple_of(h * 128, 128), 128)] = head(mb, h)
            return 0
        lax.fori_loop(lo // 2, hi // 2, step, 0)

    def o_copy(mb, half, core):
        cs = pl.ds(half * 1024, 1024)
        return pltpu.make_async_remote_copy(
            src_ref=oall.at[mb, pl.ds(pl.multiple_of(core * BLK, BLK), BLK), cs],
            dst_ref=oin.at[pl.ds(mb * BLK, BLK), cs],
            send_sem=os_.at[mb, half], recv_sem=or_.at[mb, half], device_id=partner, device_id_type=MESH)

    with jax.named_scope("pass1"):
        pass_on((0, 1))
    with jax.named_scope("take1"):
        take(0, (0, 1))
    with jax.named_scope("heads1a"):
        heads(0, 0, 8)
    with jax.named_scope("pass2"):
        pass_on((2,))
    o_copy(0, 0, pk).start()
    with jax.named_scope("heads1b"):
        heads(0, 8, 16)
    o_copy(0, 1, pk).start()
    with jax.named_scope("take2"):
        take(1, (2,))
    with jax.named_scope("heads2a"):
        heads(1, 0, 8)
    o_copy(1, 0, pk).start()
    with jax.named_scope("heads2b"):
        heads(1, 8, 16)
    o_copy(1, 1, pk).start()

    with jax.named_scope("wait_wo"):
        for cp in l_wo:
            cp.wait()
    orow = pl.ds(pl.multiple_of(k * BLK, BLK), BLK)
    mine = jnp.concatenate([oall[0, orow], oall[1, orow]], axis=0)
    w_mine = pl.ds(pl.multiple_of(k * 2048, 2048), 2048)
    w_other = pl.ds(pl.multiple_of(pk * 2048, 2048), 2048)
    with jax.named_scope("out_mine"):
        acc = jnp.dot(mine, wo_v[w_mine], preferred_element_type=F32)
    for mb in range(2):
        for half in range(2):
            o_copy(mb, half, pk).wait_recv()
    with jax.named_scope("out_other"):
        acc = acc + jnp.dot(oin[...], wo_v[w_other], preferred_element_type=F32)
    y[...] = acc.astype(BF16)

    for item in range(3):
        for j in (3, 2, 1):
            @pl.when(c + j < NCHIP)
            def _():
                direct(item, j).wait_send()

        def drain(j, _):
            forward(item, c - j).wait_send()
            return 0
        lax.fori_loop(0, c + 1, drain, 0)
    for i in range(2):
        q_copy(i, k).wait_send()
    for mb in range(2):
        for half in range(2):
            o_copy(mb, half, pk).wait_send()


def store_body(y, y1, y2, sem):
    for i, out in enumerate((y1, y2)):
        pltpu.make_async_copy(y.at[pl.ds(i * BLK, BLK)], out, sem.at[i]).start()
    for i, out in enumerate((y1, y2)):
        pltpu.make_async_copy(y.at[pl.ds(i * BLK, BLK)], out, sem.at[i]).wait()


def store(y):
    any_spec = pl.BlockSpec(memory_space=pl.ANY)
    return pl.pallas_call(
        store_body,
        out_shape=(jax.ShapeDtypeStruct((BLK, D_MODEL), BF16),) * 2,
        in_specs=[any_spec],
        out_specs=(any_spec,) * 2,
        scratch_shapes=[pltpu.SemaphoreType.DMA((2,))],
        compiler_params=pltpu.CompilerParams(vmem_limit_bytes=2**20),
    )(y)


def solution(mesh):
    tok_spec = P(('dp', 'sp'), None)
    idx_spec = P(('dp', 'sp'))
    any_spec = pl.BlockSpec(memory_space=pl.ANY)
    vmem_spec = pl.BlockSpec(memory_space=pltpu.VMEM)

    def local_body(x_one, seg_one, pos_one, x_two, seg_two, pos_two, w_qdown, gain_q, w_qup, w_kvdown, gain_kv, w_kvup, w_out):
        dma = pltpu.SemaphoreType.DMA
        call = pl.pallas_call(
            body,
            out_shape=jax.ShapeDtypeStruct((CHIP, D_MODEL), BF16),
            in_specs=[pl.BlockSpec(memory_space=pltpu.HBM)] * 11,
            out_specs=vmem_spec,
            scratch_shapes=[
                pltpu.VMEM((CHIP, D_MODEL), BF16),
                pltpu.VMEM((2, 1, BLK), jnp.int32),
                pltpu.VMEM((D_MODEL, Q_LAT), BF16),
                pltpu.VMEM((Q_LAT,), BF16),
                pltpu.VMEM((4, Q_LAT, 768), BF16),
                pltpu.VMEM((KV_LAT + ROPE, D_MODEL), BF16),
                pltpu.VMEM((KV_LAT,), BF16),
                pltpu.VMEM((4, KV_LAT, 1024), BF16),
                pltpu.VMEM((4096, D_MODEL), BF16),
                pltpu.VMEM((2, TOK, KV_LAT), BF16),
                pltpu.VMEM((TOK, 128), BF16),
                pltpu.VMEM((2 * CHIP, Q_LAT), BF16),
                pltpu.VMEM((3, 2 * CHIP, 128), F32),
                pltpu.VMEM((2, HEADS, CHIP, 256), BF16),
                pltpu.VMEM((2, HEADS, TOK, 256), BF16),
                pltpu.VMEM((2, CHIP, TOK), F32),
                pltpu.VMEM((2, CHIP, 2048), BF16),
                pltpu.VMEM((CHIP, 2048), BF16),
                dma((20,)), dma((3, 3)), dma((3, 4)), dma((3, 4)), dma((3, 4)),
                dma((2,)), dma((2,)), dma((2, 2)), dma((2, 2)),
            ],
            compiler_params=pltpu.CompilerParams(collective_id=0, has_side_effects=True, vmem_limit_bytes=48 * 2**20),
        )
        args = (x_one, pos_one.reshape(1, BLK), x_two, pos_two.reshape(1, BLK), w_qdown, gain_q, w_qup,
                w_kvdown.T, gain_kv, w_kvup, w_out)
        y = call(*(pltpu.with_memory_space_constraint(a, pltpu.HBM) for a in args))
        return store(y)

    return jax.shard_map(local_body, mesh=mesh,
                         in_specs=(tok_spec, idx_spec, idx_spec, tok_spec, idx_spec, idx_spec, P(), P(), P(), P(), P(), P(), P()),
                         out_specs=(tok_spec, tok_spec), check_vma=False)
```

profile of v0, /device:TPU:6, one launch (start us, length us, event | category | flops | bytes accessed | tf_op | source)
XLA Modules:
  0.0 34.2 jit_solution(14895333980019656438)
XLA Ops:
  0.6 32.8 %shard_map.122.y = bf16[128,1792]{1,0:T(8,128)(2,1)S(1)} custom-call(bf16[64,1792]{1,0:T(8,128)(2,1)} %x1.1, s32[1,64]{1,0:T(1,128)} %bitcast.4, bf16[64,1792]{1,0:T(8,128)(2,1)} %x2.1, s32[1,64]{1,0:T(1,128)} %bitcast.5, bf16[1792,384]{1,0:T(8,128)(2,1)} %wqd.1, bf16[384]{0:T(512)(128)(2,1)} %gq.1, bf16[384,6144]{1,0:T(8,128)(2,1)} %wqu.1, ...), custom_call_target="tpu_custom_call" | custom-call | tf_op jit(solution)/shard_map/pallas_call | solution.py:391
  33.4 0.8 %shard_map.123 = (bf16[64,1792]{1,0:T(8,128)(2,1)}, bf16[64,1792]{1,0:T(8,128)(2,1)}) custom-call(bf16[128,1792]{1,0:T(8,128)(2,1)S(1)} %shard_map.122.y), custom_call_target="tpu_custom_call" | custom-call | tf_op jit(solution)/shard_map/pallas_call | solution.py:342
where the time goes:
time: 34.5 us; the launch traced here: 34.2 us
  Pallas kernels  33.6 us (97%)
  between operations  0.64 us (2%)
    pallas_call x1, Pallas kernels, local_body(): y = call(*(pltpu.with_memory_space_constraint(a, pltpu.HBM) for a in args))  32.8 us
    pallas_call x1, Pallas kernels, store(): pl.pallas_call(store_body, out_shape=(jax.ShapeDtypeStruct((BLK, D_MODEL)...  0.78 us

commit v1 on v0

--- a/solution.py
+++ b/solution.py
@@ -33,8 +33,9 @@
 
 def body(x1, p1, x2, p2, wqd, gq, wqu, wkvd, gkv, wkvu, wo, y,
          xv, posv, wqd_v, gq_v, wqu_v, wkvd_v, gkv_v, wkvu_v, wo_v,
-         kvlat, ropeb, qlat, tabs, qbuf, kvb, bias, oall, oin,
+         kvlat0, kvlat1, qlat, tabs, qbuf, kvb, krope, bias, oall, oin, acc,
          lsem, ds, dr, fs, fr, qs, qr, os_, or_):
+    kvlat = (kvlat0, kvlat1)
     sp = lax.axis_index("sp")
     dp = lax.axis_index("dp")
     k = lax.rem(sp, 2)
@@ -56,12 +57,12 @@
     l_p1 = local(p1, posv.at[0], 2)
     l_p2 = local(p2, posv.at[1], 3)
     l_gkv = local(gkv, gkv_v, 4)
-    l_wkvd = local(wkvd, wkvd_v, 5)
+    l_wkvd = [local(wkvd.at[pl.ds(a, n)], wkvd_v.at[pl.ds(a, n)], i) for a, n, i in ((256, 320, 5), (0, 256, 20))]
     l_gq = local(gq, gq_v, 6)
     l_wqd = local(wqd, wqd_v, 7)
     l_wkvu = [local(wkvu.at[:, pl.ds(pl.multiple_of(k * 4096 + i * 1024, 1024), 1024)], wkvu_v.at[i], 8 + i) for i in range(4)]
     l_wqu = [local(wqu.at[:, pl.ds(pl.multiple_of(k * 3072 + i * 768, 256), 768)], wqu_v.at[i], 12 + i) for i in range(4)]
-    l_wo = [local(wo.at[pl.ds(i * 1024, 1024)], wo_v.at[pl.ds(i * 1024, 1024)], 16 + i) for i in range(4)]
+    l_wo = [local(wo.at[pl.ds(pl.multiple_of(lax.rem(k * 2048 + i * 1024, 4096), 1024), 1024)], wo_v.at[pl.ds(i * 1024, 1024)], 16 + i) for i in range(4)]
 
     barrier = pltpu.get_barrier_semaphore()
     pl.semaphore_signal(barrier, inc=1, device_id=partner, device_id_type=MESH)
@@ -71,7 +72,8 @@
     for b in range(1, NCHIP):
         @pl.when(c < b)
         def _():
-            ropeb[pl.ds(b * CHIP, CHIP)] = jnp.zeros((CHIP, 128), BF16)
+            kvlat0[pl.ds(b * CHIP, CHIP), KV_LAT:] = jnp.zeros((CHIP, 128), BF16)
+            kvlat1[pl.ds(b * CHIP, CHIP)] = jnp.zeros((CHIP, KV_LAT), BF16)
 
             def zero(h, _):
                 for mb in range(2):
@@ -106,23 +108,29 @@
         l_x1.wait()
         l_x2.wait()
         l_gkv.wait()
-        l_wkvd.wait()
-    u = lax.dot_general(xv[...], wkvd_v[...], (((1,), (1,)), ((), ())), preferred_element_type=F32)
-    ckv = norm_rows(u[:, :KV_LAT], gkv_v[...])
-    ur = u[:, KV_LAT:]
+        l_wkvd[0].wait()
+
+    def kv_down(a, n):
+        return lax.dot_general(xv[...], wkvd_v[a:a + n], (((1,), (1,)), ((), ())), preferred_element_type=F32)
+
+    u_b = kv_down(256, 320)
+    l_wkvd[1].wait()
+    u_a = kv_down(0, 256)
+    ur = u_b[:, 256:]
     kr = rot(jnp.concatenate([ur, ur], axis=1), cos_t, sin_t)
     kr = jnp.where(lo64, kr[:BLK], kr[BLK:]).astype(BF16)
 
+    ckv = norm_rows(jnp.concatenate([u_a, u_b[:, :256]], axis=1), gkv_v[...])
+
     def rows(chip, core):
         return pl.ds(pl.multiple_of(chip * CHIP + core * BLK, BLK), BLK)
 
     def part(item, chip, core):
-        r = rows(chip, core)
-        return ropeb.at[r] if item == 0 else kvlat.at[item - 1, r]
-
-    ropeb[rows(c, k)] = kr
-    kvlat[0, rows(c, k)] = ckv[:BLK]
-    kvlat[1, rows(c, k)] = ckv[BLK:]
+        return kvlat[item].at[rows(chip, core)]
+
+    kvlat[0][rows(c, k), KV_LAT:] = kr
+    kvlat[0][rows(c, k), :KV_LAT] = ckv[:BLK]
+    kvlat[1][rows(c, k)] = ckv[BLK:]
 
     with jax.named_scope("barrier"):
         pl.semaphore_wait(barrier, 4)
@@ -147,11 +155,14 @@
         return pltpu.make_async_remote_copy(src_ref=p, dst_ref=p, send_sem=fs.at[item, chip], recv_sem=fr.at[item, chip],
                                             device_id=partner, device_id_type=MESH)
 
-    for item in range(3):
+    def send(item):
         for j in (3, 2, 1):
             @pl.when(c + j < NCHIP)
             def _():
                 direct(item, j).start()
+
+    send(0)
+    for item in range(2):
         forward(item, c).start()
 
     l_gq.wait()
@@ -174,30 +185,31 @@
             for h in range(4):
                 store(i * 4 + h, kv[:, h * 256:(h + 1) * 256])
 
-    def kv_up_device(core):
-        r = rows(c, core)
+    def chip_rows(chip):
+        return pl.ds(pl.multiple_of(chip * CHIP, CHIP), CHIP)
+
+    def kv_up_own():
+        r = chip_rows(c)
 
         def store(h, val):
-            kvb[0, h, r] = val[:BLK]
-            kvb[1, h, r] = val[BLK:]
-        kv_up(jnp.concatenate([kvlat[0, r], kvlat[1, r]], axis=0), store)
-
-    def kv_up_chip(mb, chip):
-        r = pl.ds(pl.multiple_of(chip * CHIP, CHIP), CHIP)
-
+            kvb[0, h, r] = val[:CHIP]
+            kvb[1, h, r] = val[CHIP:]
+        kv_up(jnp.concatenate([kvlat0[r, :KV_LAT], kvlat1[r]], axis=0), store)
+
+    def kv_up_rows(mb, r):
         def store(h, val):
             kvb[mb, h, r] = val
-        kv_up(kvlat[mb, r], store)
+        kv_up(kvlat[mb][r, :KV_LAT], store)
 
     with jax.named_scope("wait_wkvu"):
         for cp in l_wkvu:
             cp.wait()
+    with jax.named_scope("wait_partner"):
+        for item in range(2):
+            forward_recv(item, c).wait_recv()
     with jax.named_scope("kv_own"):
-        kv_up_device(k)
-    for item in range(3):
-        forward_recv(item, c).wait_recv()
-    with jax.named_scope("kv_partner"):
-        kv_up_device(pk)
+        kv_up_own()
+    send(1)
 
     for i in range(2):
         q_copy(i, pk).wait_recv()
@@ -211,63 +223,60 @@
     for cp in l_wqu:
         cp.wait()
 
-    def q_up(i, _):
-        f = jnp.dot(qlat[...], wqu_v[i], preferred_element_type=F32)
-        cs = tabs[0]
-        sn = tabs[1]
+    def q_up(i):
+        return jnp.dot(qlat[...], wqu_v[i], preferred_element_type=F32)
+
+    def q_store(i, f):
         for pair in range(2):
             t0, t1, t2 = (f[:, pair * 384 + n * 128: pair * 384 + (n + 1) * 128] for n in range(3))
             n1 = pltpu.roll(jnp.where(lo64, t2, t1), 64, 1)
-            r = rot(jnp.where(lo64, t1, t2), cs, sn)
-            rw = pltpu.roll(r, 64, 1)
-            nopes = (t0.astype(BF16), n1.astype(BF16))
+            r = rot(jnp.where(lo64, t1, t2), tabs[0], tabs[1])
             zero = jnp.zeros_like(r)
-            ropes = ((jnp.where(lo64, r, zero).astype(BF16), jnp.where(lo64, rw, zero).astype(BF16)),
-                     (jnp.where(lo64, zero, rw).astype(BF16), jnp.where(lo64, zero, r).astype(BF16)))
+            q = ((t0.astype(BF16), jnp.where(lo64, r, zero).astype(BF16)),
+                 (n1.astype(BF16), jnp.where(lo64, zero, r).astype(BF16)))
             for odd in range(2):
                 h = i * 4 + pair * 2 + odd
                 for mb in range(2):
                     for core in range(2):
                         s = slice(core * CHIP + mb * BLK, core * CHIP + (mb + 1) * BLK)
-                        qbuf[mb, h, pl.ds(core * BLK, BLK), 0:128] = nopes[odd][s]
-                        qbuf[mb, h, pl.ds(core * BLK, BLK), 128:256] = ropes[mb][odd][s]
-        return 0
+                        for n in range(2):
+                            qbuf[mb, h, pl.ds(core * BLK, BLK), n * 128:(n + 1) * 128] = q[odd][n][s]
+
     with jax.named_scope("q_up"):
-        lax.fori_loop(0, 4, q_up, 0)
-
-    def pass_on(items):
-        def step(j, _):
-            for item in items:
-                direct_recv(item, c - j).wait_recv()
-                forward(item, c - j).start()
-            return 0
-        lax.fori_loop(1, c + 1, step, 0)
-
-    def take(mb, items):
-        def step(j, _):
-            for item in items:
-                forward_recv(item, c - j).wait_recv()
-            kv_up_chip(mb, c - j)
-            return 0
-        lax.fori_loop(1, c + 1, step, 0)
-
-    def head(mb, h):
-        kv = kvb[mb, h]
-        kcat = jnp.concatenate([kv[:, :NOPE], ropeb[...]], axis=1)
-        s = lax.dot_general(qbuf[mb, h], kcat, (((1,), (1,)), ((), ())), preferred_element_type=F32)
-        s = jnp.minimum(s, bias[mb])
-        m = jnp.max(s, axis=1, keepdims=True)
-        e = jnp.exp2((s - m) * SCALE2)
-        p = (e * (1.0 / jnp.sum(e, axis=1, keepdims=True))).astype(BF16)
-        return jnp.dot(p, kv[:, NOPE:], preferred_element_type=F32).astype(BF16)
-
-    def heads(mb, lo, hi):
-        def step(i, _):
-            for u_ in range(2):
-                h = i * 2 + u_
-                oall[mb, :, pl.ds(pl.multiple_of(h * 128, 128), 128)] = head(mb, h)
-            return 0
-        lax.fori_loop(lo // 2, hi // 2, step, 0)
+        prev = q_up(0)
+        for i in range(4):
+            nxt = q_up(i + 1) if i < 3 else None
+            q_store(i, prev)
+            prev = nxt
+
+    def each_earlier_chip(step):
+        lax.fori_loop(1, c + 1, lambda j, _: (step(c - j), 0)[1], 0)
+
+    def pass_on(item):
+        def step(chip):
+            direct_recv(item, chip).wait_recv()
+            forward(item, chip).start()
+        each_earlier_chip(step)
+
+    def spread_rope():
+        r = kvlat0[:, KV_LAT:]
+        krope[0] = jnp.concatenate([r[:, :ROPE], r[:, :ROPE]], axis=1)
+        krope[1] = jnp.concatenate([r[:, ROPE:], r[:, ROPE:]], axis=1)
+
+    def heads(mb):
+        scores = []
+        for h in range(HEADS):
+            kcat = jnp.concatenate([kvb[mb, h, :, :NOPE], krope[mb]], axis=1)
+            scores.append(lax.dot_general(qbuf[mb, h], kcat, (((1,), (1,)), ((), ())), preferred_element_type=F32))
+        probs = []
+        for s in scores:
+            s = jnp.minimum(s, bias[mb])
+            m = jnp.max(s, axis=1, keepdims=True)
+            e = jnp.exp2((s - m) * SCALE2)
+            probs.append((e * (1.0 / jnp.sum(e, axis=1, keepdims=True))).astype(BF16))
+        for h in range(HEADS):
+            o = jnp.dot(probs[h], kvb[mb, h, :, NOPE:], preferred_element_type=F32)
+            oall[mb, :, h * 128:(h + 1) * 128] = o.astype(BF16)
 
     def o_copy(mb, half, core):
         cs = pl.ds(half * 1024, 1024)
@@ -277,43 +286,45 @@
             send_sem=os_.at[mb, half], recv_sem=or_.at[mb, half], device_id=partner, device_id_type=MESH)
 
     with jax.named_scope("pass1"):
-        pass_on((0, 1))
-    with jax.named_scope("take1"):
-        take(0, (0, 1))
-    with jax.named_scope("heads1a"):
-        heads(0, 0, 8)
+        pass_on(0)
+
+    def take_one(chip):
+        with jax.named_scope("take1_wait"):
+            forward_recv(0, chip).wait_recv()
+        with jax.named_scope("take1"):
+            kv_up_rows(0, chip_rows(chip))
+    each_earlier_chip(take_one)
     with jax.named_scope("pass2"):
-        pass_on((2,))
-    o_copy(0, 0, pk).start()
-    with jax.named_scope("heads1b"):
-        heads(0, 8, 16)
-    o_copy(0, 1, pk).start()
+        pass_on(1)
+    spread_rope()
+    with jax.named_scope("heads1"):
+        heads(0)
+    for half in range(2):
+        o_copy(0, half, pk).start()
+    with jax.named_scope("take2_wait"):
+        each_earlier_chip(lambda chip: forward_recv(1, chip).wait_recv())
     with jax.named_scope("take2"):
-        take(1, (2,))
-    with jax.named_scope("heads2a"):
-        heads(1, 0, 8)
-    o_copy(1, 0, pk).start()
-    with jax.named_scope("heads2b"):
-        heads(1, 8, 16)
-    o_copy(1, 1, pk).start()
-
-    with jax.named_scope("wait_wo"):
+        @pl.when(c > 0)
+        def _():
+            kv_up_rows(1, pl.ds(0, 3 * CHIP))
+    with jax.named_scope("heads2"):
+        heads(1)
+    for half in range(2):
+        o_copy(1, half, pk).start()
+
+    with jax.named_scope("out"):
         for cp in l_wo:
             cp.wait()
-    orow = pl.ds(pl.multiple_of(k * BLK, BLK), BLK)
-    mine = jnp.concatenate([oall[0, orow], oall[1, orow]], axis=0)
-    w_mine = pl.ds(pl.multiple_of(k * 2048, 2048), 2048)
-    w_other = pl.ds(pl.multiple_of(pk * 2048, 2048), 2048)
-    with jax.named_scope("out_mine"):
-        acc = jnp.dot(mine, wo_v[w_mine], preferred_element_type=F32)
-    for mb in range(2):
-        for half in range(2):
+        for mb, half in ((0, 0), (0, 1), (1, 0)):
             o_copy(mb, half, pk).wait_recv()
-    with jax.named_scope("out_other"):
-        acc = acc + jnp.dot(oin[...], wo_v[w_other], preferred_element_type=F32)
-    y[...] = acc.astype(BF16)
-
-    for item in range(3):
+        orow = pl.ds(pl.multiple_of(k * BLK, BLK), BLK)
+        mine = jnp.concatenate([oall[0, orow], oall[1, orow]], axis=0)
+        acc[...] = jnp.dot(jnp.concatenate([mine, oin[:, :1024]], axis=1), wo_v[0:3072], preferred_element_type=F32)
+    with jax.named_scope("out_last"):
+        o_copy(1, 1, pk).wait_recv()
+        y[...] = (acc[...] + jnp.dot(oin[:, 1024:], wo_v[3072:], preferred_element_type=F32)).astype(BF16)
+
+    for item in range(2):
         for j in (3, 2, 1):
             @pl.when(c + j < NCHIP)
             def _():
@@ -372,19 +383,21 @@
                 pltpu.VMEM((KV_LAT,), BF16),
                 pltpu.VMEM((4, KV_LAT, 1024), BF16),
                 pltpu.VMEM((4096, D_MODEL), BF16),
-                pltpu.VMEM((2, TOK, KV_LAT), BF16),
-                pltpu.VMEM((TOK, 128), BF16),
+                pltpu.VMEM((TOK, KV_LAT + 128), BF16),
+                pltpu.VMEM((TOK, KV_LAT), BF16),
                 pltpu.VMEM((2 * CHIP, Q_LAT), BF16),
                 pltpu.VMEM((3, 2 * CHIP, 128), F32),
                 pltpu.VMEM((2, HEADS, CHIP, 256), BF16),
                 pltpu.VMEM((2, HEADS, TOK, 256), BF16),
+                pltpu.VMEM((2, TOK, 128), BF16),
                 pltpu.VMEM((2, CHIP, TOK), F32),
                 pltpu.VMEM((2, CHIP, 2048), BF16),
                 pltpu.VMEM((CHIP, 2048), BF16),
-                dma((20,)), dma((3, 3)), dma((3, 4)), dma((3, 4)), dma((3, 4)),
+                pltpu.VMEM((CHIP, D_MODEL), F32),
+                dma((21,)), dma((2, 3)), dma((2, 4)), dma((2, 4)), dma((2, 4)),
                 dma((2,)), dma((2,)), dma((2, 2)), dma((2, 2)),
             ],
-            compiler_params=pltpu.CompilerParams(collective_id=0, has_side_effects=True, vmem_limit_bytes=48 * 2**20),
+            compiler_params=pltpu.CompilerParams(collective_id=0, has_side_effects=True, vmem_limit_bytes=52 * 2**20),
         )
         args = (x_one, pos_one.reshape(1, BLK), x_two, pos_two.reshape(1, BLK), w_qdown, gain_q, w_qup,
                 w_kvdown.T, gain_kv, w_kvup, w_out)

time: 34.5 us -> 23.3 us (0.68)
  Pallas kernels: 33.6 us -> 22.5 us
    pallas_call x1, Pallas kernels: 32.8 us -> 21.7 us  [local_body(): y = call(*(pltpu.with_memory_space_constraint(a, pltpu.HBM) for a in args))]
where the time goes in v1:
time: 23.3 us; the launch traced here: 23.1 us
  Pallas kernels  22.5 us (97%)
  between operations  0.64 us (3%)
    pallas_call x1, Pallas kernels, local_body(): y = call(*(pltpu.with_memory_space_constraint(a, pltpu.HBM) for a in args))  21.7 us
    pallas_call x1, Pallas kernels, store(): pl.pallas_call(store_body, out_shape=(jax.ShapeDtypeStruct((BLK, D_MODEL)...  0.78 us

profile of v1, /device:TPU:6, one launch (start us, length us, event | category | flops | bytes accessed | tf_op | source)
XLA Modules:
  0.0 23.1 jit_solution(7122654552212558517)
XLA Ops:
  0.6 21.7 %shard_map.122.y = bf16[128,1792]{1,0:T(8,128)(2,1)S(1)} custom-call(bf16[64,1792]{1,0:T(8,128)(2,1)} %x1.1, s32[1,64]{1,0:T(1,128)} %bitcast.4, bf16[64,1792]{1,0:T(8,128)(2,1)} %x2.1, s32[1,64]{1,0:T(1,128)} %bitcast.5, bf16[1792,384]{1,0:T(8,128)(2,1)} %wqd.1, bf16[384]{0:T(512)(128)(2,1)} %gq.1, bf16[384,6144]{1,0:T(8,128)(2,1)} %wqu.1, ...), custom_call_target="tpu_custom_call" | custom-call | tf_op jit(solution)/shard_map/pallas_call | solution.py:404
  22.3 0.8 %shard_map.123 = (bf16[64,1792]{1,0:T(8,128)(2,1)}, bf16[64,1792]{1,0:T(8,128)(2,1)}) custom-call(bf16[128,1792]{1,0:T(8,128)(2,1)S(1)} %shard_map.122.y), custom_call_target="tpu_custom_call" | custom-call | tf_op jit(solution)/shard_map/pallas_call | solution.py:353

commit v2 on v1

v2 whole, which is shorter than its diff:
```python
import jax
import jax.numpy as jnp
from jax import lax
from jax.experimental import pallas as pl
from jax.experimental.pallas import tpu as pltpu
from jax.sharding import PartitionSpec as P

MESH = pl.DeviceIdType.MESH
F32 = jnp.float32
BF16 = jnp.bfloat16

D_MODEL = 1792
Q_LAT = 384
KV_LAT = 512
ROPE = 64
NOPE = 128
HEADS = 16
BLK = 64
CHIP = 2 * BLK
TOK = 512
NCHIP = 4
LN_BASE = 9.210340371976184
EPS = 1e-6
LEAD = 4
K_A = 1024
SCALE2 = 192 ** -0.5 * 1.4426950408889634
NEG = -1e30
BIG = 3.0e38


def norm_rows(z, gain):
    ms = jnp.mean(z * z, axis=-1, keepdims=True)
    return (z * lax.rsqrt(ms + EPS) * gain.astype(F32)[None, :]).astype(BF16)


def body(x1, p1, x2, p2, wqd, gq, wqu, wkvd, gkv, wkvu, wo, y,
         xv, posv, wqd_v, gq_v, wqu_v, wkvd_v, gkv_v, wkvu_v, wo_v,
         kvlat0, kvlat1, qlat, tabs, qbuf, kheld, kT, vb, kropeT, bias, oall, oin, acc, usum,
         lsem, ds, dr, fs, fr, qs, qr, os_, or_):
    kvlat = (kvlat0, kvlat1)
    sp = lax.axis_index("sp")
    dp = lax.axis_index("dp")
    k = lax.rem(sp, 2)
    c = lax.div(sp, 2)
    pk = 1 - k

    def dev(chip, core):
        return (dp, chip * 2 + core)

    partner = dev(c, pk)

    def local(src, dst, i):
        cp = pltpu.make_async_copy(src, dst, lsem.at[i])
        cp.start()
        return cp

    local(p1, posv.at[0], 0)
    local(p2, posv.at[1], 0)
    local(x1, xv.at[pl.ds(0, BLK)], 1)
    local(x2, xv.at[pl.ds(BLK, BLK)], 1)
    l_wkvd = [local(wkvd.at[:, pl.ds(a, n)], wkvd_v.at[:, pl.ds(a, n)], i) for a, n, i in ((0, K_A, 2), (K_A, D_MODEL - K_A, 3))]
    l_gkv = local(gkv, gkv_v, 4)
    l_gq = local(gq, gq_v, 5)
    l_wqd = local(wqd, wqd_v, 6)
    l_wkvu = local(wkvu.at[:, pl.ds(pl.multiple_of(k * 4096, 4096), 4096)], wkvu_v, 7)
    l_wqu = local(wqu.at[:, pl.ds(pl.multiple_of(k * 3072, 1024), 3072)], wqu_v, 8)
    for i, core in enumerate((k, pk)):
        local(wo.at[pl.ds(pl.multiple_of(core * 2048, 2048), 2048)], wo_v.at[pl.ds(i * 2048, 2048)], 9)

    def wait_whole(ref, i):
        pltpu.make_async_copy(ref, ref, lsem.at[i]).wait()

    barrier = pltpu.get_barrier_semaphore()
    pl.semaphore_signal(barrier, inc=1, device_id=partner, device_id_type=MESH)
    for j in range(1, NCHIP):
        for core in range(2):
            pl.semaphore_signal(barrier, inc=1, device_id=dev(lax.rem(c + j, NCHIP), core), device_id_type=MESH)

    for b in range(1, NCHIP):
        @pl.when(c < b)
        def _():
            kvlat0[pl.ds(b * CHIP, CHIP), KV_LAT:] = jnp.zeros((CHIP, 128), BF16)

            def zero(h, _):
                for mb in range(2):
                    kT[mb, h, :, pl.ds(b * CHIP, CHIP)] = jnp.zeros((128, CHIP), BF16)
                    vb[mb, h, pl.ds(b * CHIP, CHIP)] = jnp.zeros((CHIP, 128), BF16)
                return 0
            lax.fori_loop(0, HEADS, zero, 0)

    lane = lax.broadcasted_iota(jnp.int32, (1, 128), 1)
    lo64 = lane < 64
    lo32 = lax.rem(lane, 64) < 32

    wait_whole(posv, 0)
    own = pl.ds(pl.multiple_of(k * CHIP, CHIP), CHIP)
    eye = lax.broadcasted_iota(jnp.int32, (BLK, BLK), 0) == lax.broadcasted_iota(jnp.int32, (BLK, BLK), 1)
    cols = [jnp.sum(jnp.where(eye, posv[mb].astype(F32), 0.0), axis=1, keepdims=True) for mb in range(2)]
    pos_col = jnp.concatenate(cols, axis=0)
    freq = jnp.exp(lax.rem(lane, 32).astype(F32) * (-LN_BASE / 32))
    ang = pos_col * freq
    cos_t = jnp.cos(ang)
    sin_t = jnp.sin(ang)
    sin_t = jnp.where(lo32, -sin_t, sin_t)
    tabs[0, own] = cos_t
    tabs[1, own] = sin_t
    tabs[2, own] = pos_col + jnp.zeros((CHIP, 128), F32)

    def rot(z, cs, sn):
        sw = jnp.where(lo32, pltpu.roll(z, 96, 1), pltpu.roll(z, 32, 1))
        return z * cs + sw * sn

    def kv_down(a, n):
        return lax.dot_general(xv[:, a:a + n], wkvd_v[:, a:a + n], (((1,), (1,)), ((), ())), preferred_element_type=F32)

    with jax.named_scope("wait_x"):
        wait_whole(xv, 1)
        l_wkvd[0].wait()
    usum[...] = kv_down(0, K_A)
    with jax.named_scope("wait_wd"):
        l_wkvd[1].wait()
        l_gkv.wait()
    u = usum[...] + kv_down(K_A, D_MODEL - K_A)
    ur = u[:, KV_LAT:]
    kr = rot(jnp.concatenate([ur, ur], axis=1), cos_t, sin_t)
    kr = jnp.where(lo64, kr[:BLK], kr[BLK:]).astype(BF16)

    ckv = norm_rows(u[:, :KV_LAT], gkv_v[...])

    def rows(chip, core):
        return pl.ds(pl.multiple_of(chip * CHIP + core * BLK, BLK), BLK)

    def chip_rows(chip):
        return pl.ds(pl.multiple_of(chip * CHIP, CHIP), CHIP)

    def part(item, chip, core):
        return kvlat[item].at[rows(chip, core)]

    kvlat[0][rows(c, k), KV_LAT:] = kr
    kvlat[0][rows(c, k), :KV_LAT] = ckv[:BLK]
    kvlat[1][rows(c, k)] = ckv[BLK:]

    with jax.named_scope("barrier"):
        pl.semaphore_wait(barrier, 7)

    def direct(item, j):
        p = part(item, c, k)
        return pltpu.make_async_remote_copy(src_ref=p, dst_ref=p, send_sem=ds.at[item, j - 1], recv_sem=dr.at[item, j - 1],
                                            device_id=dev(c + j, 1), device_id_type=MESH)

    def direct_recv(item, j):
        p = kvlat[item].at[chip_rows(c - j)]
        return pltpu.make_async_remote_copy(src_ref=p, dst_ref=p, send_sem=ds.at[item, 0], recv_sem=dr.at[item, j - 1],
                                            device_id=partner, device_id_type=MESH)

    def share(item, core):
        p = part(item, c, core)
        return pltpu.make_async_remote_copy(src_ref=p, dst_ref=p, send_sem=fs.at[item, 0], recv_sem=fr.at[item, 0],
                                            device_id=partner, device_id_type=MESH)

    def forward(item, j):
        p = kvlat[item].at[chip_rows(c - j)]
        return pltpu.make_async_remote_copy(src_ref=p, dst_ref=p, send_sem=fs.at[item, j], recv_sem=fr.at[item, j],
                                            device_id=partner, device_id_type=MESH)

    def send(item):
        for j in (3, 2, 1):
            @pl.when(c + j < NCHIP)
            def _():
                direct(item, j).start()

    send(0)
    for item in range(2):
        share(item, k).start()

    l_gq.wait()
    l_wqd.wait()
    with jax.named_scope("q_down"):
        cq = jnp.dot(xv[...], wqd_v[...], preferred_element_type=F32)
        qlat[own] = norm_rows(cq, gq_v[...])

    def q_copy(i, core):
        r = pl.ds(pl.multiple_of(core * CHIP, CHIP), CHIP)
        p = qlat.at[r] if i == 0 else tabs.at[:, r]
        return pltpu.make_async_remote_copy(src_ref=p, dst_ref=p, send_sem=qs.at[i], recv_sem=qr.at[i],
                                            device_id=partner, device_id_type=MESH)

    for i in range(2):
        q_copy(i, k).start()

    def kv_up(lhs, store, turn=True):
        for i in range(4):
            kv = jnp.dot(lhs, wkvu_v[:, i * 1024:(i + 1) * 1024], preferred_element_type=F32).astype(BF16)
            for n in range(4):
                key = kv[:, n * 256:n * 256 + NOPE]
                store(i * 4 + n, key.T if turn else key, kv[:, n * 256 + NOPE:(n + 1) * 256])

    def kv_up_own():
        r = chip_rows(c)

        def store(h, key, val):
            for mb in range(2):
                kT[mb, h, :, r] = key[:, mb * CHIP:(mb + 1) * CHIP]
                vb[mb, h, r] = val[mb * CHIP:(mb + 1) * CHIP]
        kv_up(jnp.concatenate([kvlat0[r, :KV_LAT], kvlat1[r]], axis=0), store)

    def kv_up_device(core, store_key):
        r = rows(c, core)

        def store(h, key, val):
            store_key(h, key)
            for mb in range(2):
                vb[mb, h, r] = val[mb * BLK:(mb + 1) * BLK]
        kv_up(jnp.concatenate([kvlat0[r, :KV_LAT], kvlat1[r]], axis=0), store, False)

    def hold_key(h, key):
        kheld[h] = key

    def join_key(h, key):
        for mb in range(2):
            s = slice(mb * BLK, (mb + 1) * BLK)
            kT[mb, h, :, chip_rows(c)] = jnp.concatenate([key[s], kheld[h, s]], axis=0).T

    def kv_up_first(r):
        def store(h, key, val):
            kT[0, h, :, r] = key
            vb[0, h, r] = val
        kv_up(kvlat0[r, :KV_LAT], store)

    with jax.named_scope("wait_wkvu"):
        l_wkvu.wait()
    def wait_share():
        with jax.named_scope("wait_partner"):
            for item in range(2):
                share(item, pk).wait_recv()

    with jax.named_scope("kv_own"):
        @pl.when(k == 0)
        def _():
            wait_share()
            kv_up_own()

        @pl.when(k == 1)
        def _():
            kv_up_device(k, hold_key)
            wait_share()
            kv_up_device(pk, join_key)

    for i in range(2):
        q_copy(i, pk).wait_recv()
    for mb in range(2):
        for core in range(2):
            pos = tabs[2, pl.ds(core * CHIP + mb * BLK, BLK), 0:1].astype(jnp.int32)
            qi = c * CHIP + core * BLK + lax.broadcasted_iota(jnp.int32, (BLK, TOK), 0)
            ki = lax.broadcasted_iota(jnp.int32, (BLK, TOK), 1)
            keep = jnp.logical_and(ki <= qi, ki >= qi - pos)
            bias[mb, pl.ds(core * BLK, BLK)] = jnp.where(keep, BIG, NEG)
    l_wqu.wait()

    def q_up(i):
        return jnp.dot(qlat[...], wqu_v[:, i * 768:(i + 1) * 768], preferred_element_type=F32)

    def q_store(i, f):
        for pair in range(2):
            t0, t1, t2 = (f[:, pair * 384 + n * 128: pair * 384 + (n + 1) * 128] for n in range(3))
            n1 = pltpu.roll(jnp.where(lo64, t2, t1), 64, 1)
            r = rot(jnp.where(lo64, t1, t2), tabs[0], tabs[1])
            zero = jnp.zeros_like(r)
            q = ((t0.astype(BF16), jnp.where(lo64, r, zero).astype(BF16)),
                 (n1.astype(BF16), jnp.where(lo64, zero, r).astype(BF16)))
            for odd in range(2):
                h = i * 4 + pair * 2 + odd
                for mb in range(2):
                    for core in range(2):
                        s = slice(core * CHIP + mb * BLK, core * CHIP + (mb + 1) * BLK)
                        for n in range(2):
                            qbuf[mb, h, pl.ds(core * BLK, BLK), n * 128:(n + 1) * 128] = q[odd][n][s]

    def nth(i):
        return jnp.where(jnp.logical_and(c == 3, i > 1), 5 - i, i)

    def each_earlier_chip(step):
        lax.fori_loop(1, c + 1, lambda i, _: (step(i, nth(i)), 0)[1], 0)

    def pass_on(item, j):
        direct_recv(item, j).wait_recv()
        forward(item, j).start()

    with jax.named_scope("q_up"):
        prev = q_up(0)
        for i in range(4):
            nxt = q_up(i + 1) if i < 3 else None
            q_store(i, prev)
            prev = nxt

    with jax.named_scope("pass_on"):
        for j, at in ((1, c > 0), (3, c == 3)):
            @pl.when(jnp.logical_and(k == 1, at))
            def _():
                pass_on(0, j)

    send(1)

    def o_copy(mb, half):
        cs = pl.ds(half * 1024, 1024)
        return pltpu.make_async_remote_copy(
            src_ref=oall.at[mb, pl.ds(pl.multiple_of(pk * BLK, BLK), BLK), cs], dst_ref=oin.at[pl.ds(mb * BLK, BLK), cs],
            send_sem=os_.at[0], recv_sem=or_.at[mb * half], device_id=partner, device_id_type=MESH)

    def o_bytes(n, i):
        p = oin.at[pl.ds(0, n)]
        return pltpu.make_async_remote_copy(src_ref=p, dst_ref=p, send_sem=os_.at[0], recv_sem=or_.at[i],
                                            device_id=partner, device_id_type=MESH)

    def spread_rope():
        r = kvlat0[:, KV_LAT:].T
        for mb in range(2):
            half = r[mb * ROPE:(mb + 1) * ROPE]
            kropeT[mb] = jnp.concatenate([half, half], axis=0)

    def heads(mb, lo, hi, beside=lambda h: None):
        scores = []
        for h in range(lo, hi):
            kcat = jnp.concatenate([kT[mb, h], kropeT[mb]], axis=0)
            scores.append(jnp.dot(qbuf[mb, h], kcat, preferred_element_type=F32))
            beside(h)
        probs = []
        for s in scores:
            s = jnp.minimum(s, bias[mb])
            m = jnp.max(s, axis=1, keepdims=True)
            e = jnp.exp2((s - m) * SCALE2)
            probs.append((e * (1.0 / jnp.sum(e, axis=1, keepdims=True))).astype(BF16))
        for h in range(lo, hi):
            o = jnp.dot(probs[h - lo], vb[mb, h], preferred_element_type=F32)
            oall[mb, :, h * 128:(h + 1) * 128] = o.astype(BF16)
            if h % 8 == 7:
                o_copy(mb, h // 8).start()

    def kv_up_second(n):
        def two(i):
            kv = jnp.dot(kvlat1[0:n], wkvu_v[:, i * 512:(i + 1) * 512], preferred_element_type=F32).astype(BF16)
            for h in range(2):
                kT[1, 2 * i + h, :, 0:n] = kv[:, h * 256:h * 256 + NOPE].T
                vb[1, 2 * i + h, 0:n] = kv[:, h * 256 + NOPE:(h + 1) * 256]
        return two

    def take(item, j):
        with jax.named_scope("take_wait"):
            @pl.when(k == 0)
            def _():
                forward(item, j).wait_recv()

    def pass_if(at, item, j):
        @pl.when(jnp.logical_and(k == 1, at))
        def _():
            pass_on(item, j)

    @pl.when(c > 0)
    def _():
        take(0, 1)
        with jax.named_scope("take1"):
            kv_up_first(chip_rows(c - 1))

    @pl.when(c == 2)
    def _():
        pass_if(True, 0, 2)
        take(0, 2)
        with jax.named_scope("take1"):
            kv_up_first(pl.ds(0, CHIP))

    @pl.when(c == 3)
    def _():
        pass_if(True, 0, 2)
        take(0, 3)
        take(0, 2)
        with jax.named_scope("take1"):
            kv_up_first(pl.ds(0, 2 * CHIP))
    spread_rope()
    with jax.named_scope("heads1a"):
        heads(0, 0, 8)

    def take_later(i, j):
        pass_if(True, 1, j)
        take(1, j)

    @pl.when(c == 3)
    def _():
        with jax.named_scope("take2_wait"):
            each_earlier_chip(take_later)
        with jax.named_scope("heads1b"):
            two = kv_up_second(3 * CHIP)
            heads(0, 8, 16, lambda h: two(h - 8))

    @pl.when(c < 3)
    def _():
        with jax.named_scope("heads1c"):
            heads(0, 8, 16)
        with jax.named_scope("take2_wait"):
            each_earlier_chip(take_later)
        for n in (1, 2):
            @pl.when(c == n)
            def _():
                with jax.named_scope("take2"):
                    two = kv_up_second(n * CHIP)
                    for i in range(8):
                        two(i)
    with jax.named_scope("heads2"):
        heads(1, 0, 16)

    with jax.named_scope("out"):
        wait_whole(wo_v, 9)
        orow = pl.ds(pl.multiple_of(k * BLK, BLK), BLK)
        mine = jnp.concatenate([oall[0, orow], oall[1, orow]], axis=0)
        acc[...] = jnp.dot(mine, wo_v[0:2048], preferred_element_type=F32)
    with jax.named_scope("out_b"):
        o_bytes(96, 0).wait_recv()
        acc[...] += jnp.dot(oin[:, :1024], wo_v[2048:3072], preferred_element_type=F32)
    with jax.named_scope("out_last"):
        o_bytes(32, 1).wait_recv()
        y[...] = (acc[...] + jnp.dot(oin[:, 1024:], wo_v[3072:], preferred_element_type=F32)).astype(BF16)

    for item in range(2):
        for j in (3, 2, 1):
            @pl.when(c + j < NCHIP)
            def _():
                direct(item, j).wait_send()

        share(item, k).wait_send()

        @pl.when(k == 1)
        def _():
            each_earlier_chip(lambda i, j: forward(item, j).wait_send())
    for i in range(2):
        q_copy(i, k).wait_send()
    o_bytes(CHIP, 0).wait_send()


def store_body(y, y1, y2, sem):
    for i, out in enumerate((y1, y2)):
        pltpu.make_async_copy(y.at[pl.ds(i * BLK, BLK)], out, sem.at[i]).start()
    for i, out in enumerate((y1, y2)):
        pltpu.make_async_copy(y.at[pl.ds(i * BLK, BLK)], out, sem.at[i]).wait()


def store(y):
    any_spec = pl.BlockSpec(memory_space=pl.ANY)
    return pl.pallas_call(
        store_body,
        out_shape=(jax.ShapeDtypeStruct((BLK, D_MODEL), BF16),) * 2,
        in_specs=[any_spec],
        out_specs=(any_spec,) * 2,
        scratch_shapes=[pltpu.SemaphoreType.DMA((2,))],
        compiler_params=pltpu.CompilerParams(vmem_limit_bytes=2**20),
    )(y)


def solution(mesh):
    tok_spec = P(('dp', 'sp'), None)
    idx_spec = P(('dp', 'sp'))
    any_spec = pl.BlockSpec(memory_space=pl.ANY)
    vmem_spec = pl.BlockSpec(memory_space=pltpu.VMEM)

    def local_body(x_one, seg_one, pos_one, x_two, seg_two, pos_two, w_qdown, gain_q, w_qup, w_kvdown, gain_kv, w_kvup, w_out):
        dma = pltpu.SemaphoreType.DMA
        call = pl.pallas_call(
            body,
            out_shape=jax.ShapeDtypeStruct((CHIP, D_MODEL), BF16),
            in_specs=[pl.BlockSpec(memory_space=pltpu.HBM)] * 11,
            out_specs=vmem_spec,
            scratch_shapes=[
                pltpu.VMEM((CHIP, D_MODEL), BF16),
                pltpu.VMEM((2, 1, BLK), jnp.int32),
                pltpu.VMEM((D_MODEL, Q_LAT), BF16),
                pltpu.VMEM((Q_LAT,), BF16),
                pltpu.VMEM((Q_LAT, 3072), BF16),
                pltpu.VMEM((KV_LAT + ROPE, D_MODEL), BF16),
                pltpu.VMEM((KV_LAT,), BF16),
                pltpu.VMEM((KV_LAT, 4096), BF16),
                pltpu.VMEM((4096, D_MODEL), BF16),
                pltpu.VMEM((TOK, KV_LAT + 128), BF16),
                pltpu.VMEM((TOK, KV_LAT), BF16),
                pltpu.VMEM((2 * CHIP, Q_LAT), BF16),
                pltpu.VMEM((3, 2 * CHIP, 128), F32),
                pltpu.VMEM((2, HEADS, CHIP, 256), BF16),
                pltpu.VMEM((HEADS, CHIP, 128), BF16),
                pltpu.VMEM((2, HEADS, 128, TOK), BF16),
                pltpu.VMEM((2, HEADS, TOK, 128), BF16),
                pltpu.VMEM((2, 128, TOK), BF16),
                pltpu.VMEM((2, CHIP, TOK), F32),
                pltpu.VMEM((2, CHIP, 2048), BF16),
                pltpu.VMEM((CHIP, 2048), BF16),
                pltpu.VMEM((CHIP, D_MODEL), F32),
                pltpu.VMEM((CHIP, KV_LAT + ROPE), F32),
                dma((10,)), dma((2, 3)), dma((2, 3)), dma((2, 4)), dma((2, 4)),
                dma((2,)), dma((2,)), dma((1,)), dma((2,)),
            ],
            compiler_params=pltpu.CompilerParams(collective_id=0, has_side_effects=True, vmem_limit_bytes=52 * 2**20),
        )
        args = (x_one, pos_one.reshape(1, BLK), x_two, pos_two.reshape(1, BLK), w_qdown, gain_q, w_qup,
                w_kvdown.T, gain_kv, w_kvup, w_out)
        y = call(*(pltpu.with_memory_space_constraint(a, pltpu.HBM) for a in args))
        return store(y)

    return jax.shard_map(local_body, mesh=mesh,
                         in_specs=(tok_spec, idx_spec, idx_spec, tok_spec, idx_spec, idx_spec, P(), P(), P(), P(), P(), P(), P()),
                         out_specs=(tok_spec, tok_spec), check_vma=False)
```

time: 23.3 us -> 20.2 us (0.87)
  Pallas kernels: 22.5 us -> 19.3 us
    pallas_call x1, Pallas kernels: 21.7 us -> 18.5 us  [local_body(): y = call(*(pltpu.with_memory_space_constraint(a, pltpu.HBM) for a in args))]
where the time goes in v2:
time: 20.2 us; the launch traced here: 20.1 us
  Pallas kernels  19.3 us (96%)
  between operations  0.82 us (4%)
    pallas_call x1, Pallas kernels, local_body(): y = call(*(pltpu.with_memory_space_constraint(a, pltpu.HBM) for a in args))  18.5 us
    pallas_call x1, Pallas kernels, store(): pl.pallas_call(store_body, out_shape=(jax.ShapeDtypeStruct((BLK, D_MODEL)...  0.78 us

profile of v2, /device:TPU:6, one launch (start us, length us, event | category | flops | bytes accessed | tf_op | source)
XLA Modules:
  0.0 20.1 jit_solution(11043561791117314954)
XLA Ops:
  0.6 18.5 %shard_map.122.y = bf16[128,1792]{1,0:T(8,128)(2,1)S(1)} custom-call(bf16[64,1792]{1,0:T(8,128)(2,1)} %x1.1, s32[1,64]{1,0:T(1,128)} %bitcast.4, bf16[64,1792]{1,0:T(8,128)(2,1)} %x2.1, s32[1,64]{1,0:T(1,128)} %bitcast.5, bf16[1792,384]{1,0:T(8,128)(2,1)} %wqd.1, bf16[384]{0:T(512)(128)(2,1)} %gq.1, bf16[384,6144]{1,0:T(8,128)(2,1)} %wqu.1, ...), custom_call_target="tpu_custom_call" | custom-call | tf_op jit(solution)/shard_map/pallas_call | solution.py:501
  19.1 0.8 %shard_map.123 = (bf16[64,1792]{1,0:T(8,128)(2,1)}, bf16[64,1792]{1,0:T(8,128)(2,1)}) custom-call(bf16[128,1792]{1,0:T(8,128)(2,1)S(1)} %shard_map.122.y), custom_call_target="tpu_custom_call" | custom-call | tf_op jit(solution)/shard_map/pallas_call | solution.py:447

commit v3 on v2

--- a/solution.py
+++ b/solution.py
@@ -36,7 +36,7 @@
 def body(x1, p1, x2, p2, wqd, gq, wqu, wkvd, gkv, wkvu, wo, y,
          xv, posv, wqd_v, gq_v, wqu_v, wkvd_v, gkv_v, wkvu_v, wo_v,
          kvlat0, kvlat1, qlat, tabs, qbuf, kheld, kT, vb, kropeT, bias, oall, oin, acc, usum,
-         lsem, ds, dr, fs, fr, qs, qr, os_, or_):
+         lsem, sent, dr, fr, qr, or_):
     kvlat = (kvlat0, kvlat1)
     sp = lax.axis_index("sp")
     dp = lax.axis_index("dp")
@@ -59,16 +59,17 @@
     local(x1, xv.at[pl.ds(0, BLK)], 1)
     local(x2, xv.at[pl.ds(BLK, BLK)], 1)
     l_wkvd = [local(wkvd.at[:, pl.ds(a, n)], wkvd_v.at[:, pl.ds(a, n)], i) for a, n, i in ((0, K_A, 2), (K_A, D_MODEL - K_A, 3))]
-    l_gkv = local(gkv, gkv_v, 4)
-    l_gq = local(gq, gq_v, 5)
-    l_wqd = local(wqd, wqd_v, 6)
-    l_wkvu = local(wkvu.at[:, pl.ds(pl.multiple_of(k * 4096, 4096), 4096)], wkvu_v, 7)
-    l_wqu = local(wqu.at[:, pl.ds(pl.multiple_of(k * 3072, 1024), 3072)], wqu_v, 8)
-    for i, core in enumerate((k, pk)):
-        local(wo.at[pl.ds(pl.multiple_of(core * 2048, 2048), 2048)], wo_v.at[pl.ds(i * 2048, 2048)], 9)
+    l_gkv = local(gkv, gkv_v, 6)
+    l_gq = local(gq, gq_v, 7)
+    l_wqd = local(wqd, wqd_v, 4)
+    l_wkvu = local(wkvu.at[:, pl.ds(pl.multiple_of(k * 4096, 4096), 4096)], wkvu_v, 5)
 
     def wait_whole(ref, i):
         pltpu.make_async_copy(ref, ref, lsem.at[i]).wait()
+
+    def wait_bytes(ref, n, sem):
+        p = ref.at[pl.ds(0, n)]
+        pltpu.make_async_copy(p, p, sem).wait()
 
     barrier = pltpu.get_barrier_semaphore()
     pl.semaphore_signal(barrier, inc=1, device_id=partner, device_id_type=MESH)
@@ -116,6 +117,7 @@
     with jax.named_scope("wait_x"):
         wait_whole(xv, 1)
         l_wkvd[0].wait()
+    l_wqu = local(wqu.at[:, pl.ds(pl.multiple_of(k * 3072, 1024), 3072)], wqu_v, 1)
     usum[...] = kv_down(0, K_A)
     with jax.named_scope("wait_wd"):
         l_wkvd[1].wait()
@@ -145,31 +147,31 @@
 
     def direct(item, j):
         p = part(item, c, k)
-        return pltpu.make_async_remote_copy(src_ref=p, dst_ref=p, send_sem=ds.at[item, j - 1], recv_sem=dr.at[item, j - 1],
+        return pltpu.make_async_remote_copy(src_ref=p, dst_ref=p, send_sem=sent.at[0], recv_sem=dr.at[item, j - 1],
                                             device_id=dev(c + j, 1), device_id_type=MESH)
 
     def direct_recv(item, j):
         p = kvlat[item].at[chip_rows(c - j)]
-        return pltpu.make_async_remote_copy(src_ref=p, dst_ref=p, send_sem=ds.at[item, 0], recv_sem=dr.at[item, j - 1],
+        return pltpu.make_async_remote_copy(src_ref=p, dst_ref=p, send_sem=sent.at[0], recv_sem=dr.at[item, j - 1],
                                             device_id=partner, device_id_type=MESH)
 
     def share(item, core):
         p = part(item, c, core)
-        return pltpu.make_async_remote_copy(src_ref=p, dst_ref=p, send_sem=fs.at[item, 0], recv_sem=fr.at[item, 0],
+        return pltpu.make_async_remote_copy(src_ref=p, dst_ref=p, send_sem=sent.at[0], recv_sem=fr.at[0],
                                             device_id=partner, device_id_type=MESH)
 
     def forward(item, j):
         p = kvlat[item].at[chip_rows(c - j)]
-        return pltpu.make_async_remote_copy(src_ref=p, dst_ref=p, send_sem=fs.at[item, j], recv_sem=fr.at[item, j],
+        return pltpu.make_async_remote_copy(src_ref=p, dst_ref=p, send_sem=sent.at[0], recv_sem=fr.at[3 if item else 1 if j == 1 else 2],
                                             device_id=partner, device_id_type=MESH)
 
-    def send(item):
-        for j in (3, 2, 1):
-            @pl.when(c + j < NCHIP)
+    def send(item, pairs):
+        for chip, j in pairs:
+            @pl.when(c == chip)
             def _():
                 direct(item, j).start()
 
-    send(0)
+    send(0, ((0, 3), (0, 2), (0, 1), (1, 2), (1, 1), (2, 1)))
     for item in range(2):
         share(item, k).start()
 
@@ -182,7 +184,7 @@
     def q_copy(i, core):
         r = pl.ds(pl.multiple_of(core * CHIP, CHIP), CHIP)
         p = qlat.at[r] if i == 0 else tabs.at[:, r]
-        return pltpu.make_async_remote_copy(src_ref=p, dst_ref=p, send_sem=qs.at[i], recv_sem=qr.at[i],
+        return pltpu.make_async_remote_copy(src_ref=p, dst_ref=p, send_sem=sent.at[0], recv_sem=qr.at[0],
                                             device_id=partner, device_id_type=MESH)
 
     for i in range(2):
@@ -227,35 +229,14 @@
             vb[0, h, r] = val
         kv_up(kvlat0[r, :KV_LAT], store)
 
+    send(1, ((2, 1),))
     with jax.named_scope("wait_wkvu"):
         l_wkvu.wait()
+    for i, core in enumerate((k, pk)):
+        local(wo.at[pl.ds(pl.multiple_of(core * 2048, 2048), 2048)], wo_v.at[pl.ds(i * 2048, 2048)], 0)
     def wait_share():
         with jax.named_scope("wait_partner"):
-            for item in range(2):
-                share(item, pk).wait_recv()
-
-    with jax.named_scope("kv_own"):
-        @pl.when(k == 0)
-        def _():
-            wait_share()
-            kv_up_own()
-
-        @pl.when(k == 1)
-        def _():
-            kv_up_device(k, hold_key)
-            wait_share()
-            kv_up_device(pk, join_key)
-
-    for i in range(2):
-        q_copy(i, pk).wait_recv()
-    for mb in range(2):
-        for core in range(2):
-            pos = tabs[2, pl.ds(core * CHIP + mb * BLK, BLK), 0:1].astype(jnp.int32)
-            qi = c * CHIP + core * BLK + lax.broadcasted_iota(jnp.int32, (BLK, TOK), 0)
-            ki = lax.broadcasted_iota(jnp.int32, (BLK, TOK), 1)
-            keep = jnp.logical_and(ki <= qi, ki >= qi - pos)
-            bias[mb, pl.ds(core * BLK, BLK)] = jnp.where(keep, BIG, NEG)
-    l_wqu.wait()
+            wait_bytes(wqd_v, 192, fr.at[0])
 
     def q_up(i):
         return jnp.dot(qlat[...], wqu_v[:, i * 768:(i + 1) * 768], preferred_element_type=F32)
@@ -276,41 +257,53 @@
                         for n in range(2):
                             qbuf[mb, h, pl.ds(core * BLK, BLK), n * 128:(n + 1) * 128] = q[odd][n][s]
 
-    def nth(i):
-        return jnp.where(jnp.logical_and(c == 3, i > 1), 5 - i, i)
-
-    def each_earlier_chip(step):
-        lax.fori_loop(1, c + 1, lambda i, _: (step(i, nth(i)), 0)[1], 0)
-
-    def pass_on(item, j):
-        direct_recv(item, j).wait_recv()
-        forward(item, j).start()
-
-    with jax.named_scope("q_up"):
+    def queries():
+        wait_bytes(wqd_v, 384, qr.at[0])
+        for mb in range(2):
+            for core in range(2):
+                pos = tabs[2, pl.ds(core * CHIP + mb * BLK, BLK), 0:1].astype(jnp.int32)
+                qi = c * CHIP + core * BLK + lax.broadcasted_iota(jnp.int32, (BLK, TOK), 0)
+                ki = lax.broadcasted_iota(jnp.int32, (BLK, TOK), 1)
+                keep = jnp.logical_and(ki <= qi, ki >= qi - pos)
+                bias[mb, pl.ds(core * BLK, BLK)] = jnp.where(keep, BIG, NEG)
+        l_wqu.wait()
         prev = q_up(0)
         for i in range(4):
             nxt = q_up(i + 1) if i < 3 else None
             q_store(i, prev)
             prev = nxt
 
+    with jax.named_scope("kv_own"):
+        @pl.when(k == 0)
+        def _():
+            wait_share()
+            kv_up_own()
+            queries()
+
+        @pl.when(k == 1)
+        def _():
+            kv_up_device(k, hold_key)
+            wait_share()
+            kv_up_device(pk, join_key)
+            queries()
+
+    def pass_on(item, j):
+        direct_recv(item, j).wait_recv()
+        forward(item, j).start()
+
     with jax.named_scope("pass_on"):
         for j, at in ((1, c > 0), (3, c == 3)):
             @pl.when(jnp.logical_and(k == 1, at))
             def _():
                 pass_on(0, j)
 
-    send(1)
+    send(1, ((0, 3), (0, 2), (0, 1), (1, 2), (1, 1)))
 
     def o_copy(mb, half):
         cs = pl.ds(half * 1024, 1024)
         return pltpu.make_async_remote_copy(
             src_ref=oall.at[mb, pl.ds(pl.multiple_of(pk * BLK, BLK), BLK), cs], dst_ref=oin.at[pl.ds(mb * BLK, BLK), cs],
-            send_sem=os_.at[0], recv_sem=or_.at[mb * half], device_id=partner, device_id_type=MESH)
-
-    def o_bytes(n, i):
-        p = oin.at[pl.ds(0, n)]
-        return pltpu.make_async_remote_copy(src_ref=p, dst_ref=p, send_sem=os_.at[0], recv_sem=or_.at[i],
-                                            device_id=partner, device_id_type=MESH)
+            send_sem=sent.at[1], recv_sem=or_.at[mb * half], device_id=partner, device_id_type=MESH)
 
     def spread_rope():
         r = kvlat0[:, KV_LAT:].T
@@ -318,37 +311,34 @@
             half = r[mb * ROPE:(mb + 1) * ROPE]
             kropeT[mb] = jnp.concatenate([half, half], axis=0)
 
-    def heads(mb, lo, hi, beside=lambda h: None):
+    def heads(mb):
         scores = []
-        for h in range(lo, hi):
+        for h in range(HEADS):
             kcat = jnp.concatenate([kT[mb, h], kropeT[mb]], axis=0)
             scores.append(jnp.dot(qbuf[mb, h], kcat, preferred_element_type=F32))
-            beside(h)
         probs = []
         for s in scores:
             s = jnp.minimum(s, bias[mb])
             m = jnp.max(s, axis=1, keepdims=True)
             e = jnp.exp2((s - m) * SCALE2)
             probs.append((e * (1.0 / jnp.sum(e, axis=1, keepdims=True))).astype(BF16))
-        for h in range(lo, hi):
-            o = jnp.dot(probs[h - lo], vb[mb, h], preferred_element_type=F32)
+        for h in range(HEADS):
+            o = jnp.dot(probs[h], vb[mb, h], preferred_element_type=F32)
             oall[mb, :, h * 128:(h + 1) * 128] = o.astype(BF16)
             if h % 8 == 7:
                 o_copy(mb, h // 8).start()
 
     def kv_up_second(n):
-        def two(i):
-            kv = jnp.dot(kvlat1[0:n], wkvu_v[:, i * 512:(i + 1) * 512], preferred_element_type=F32).astype(BF16)
-            for h in range(2):
-                kT[1, 2 * i + h, :, 0:n] = kv[:, h * 256:h * 256 + NOPE].T
-                vb[1, 2 * i + h, 0:n] = kv[:, h * 256 + NOPE:(h + 1) * 256]
-        return two
-
-    def take(item, j):
+        def store(h, key, val):
+            kT[1, h, :, 0:n] = key
+            vb[1, h, 0:n] = val
+        kv_up(kvlat1[0:n], store)
+
+    def take(ref, n, i):
         with jax.named_scope("take_wait"):
             @pl.when(k == 0)
             def _():
-                forward(item, j).wait_recv()
+                wait_bytes(ref, n, fr.at[i])
 
     def pass_if(at, item, j):
         @pl.when(jnp.logical_and(k == 1, at))
@@ -357,82 +347,63 @@
 
     @pl.when(c > 0)
     def _():
-        take(0, 1)
+        take(kvlat0, CHIP, 1)
         with jax.named_scope("take1"):
             kv_up_first(chip_rows(c - 1))
 
-    @pl.when(c == 2)
-    def _():
-        pass_if(True, 0, 2)
-        take(0, 2)
-        with jax.named_scope("take1"):
-            kv_up_first(pl.ds(0, CHIP))
-
-    @pl.when(c == 3)
-    def _():
-        pass_if(True, 0, 2)
-        take(0, 3)
-        take(0, 2)
-        with jax.named_scope("take1"):
-            kv_up_first(pl.ds(0, 2 * CHIP))
+    for n in (2, 3):
+        @pl.when(c == n)
+        def _():
+            pass_if(True, 0, 2)
+            take(kvlat0, (n - 1) * CHIP, 2)
+            with jax.named_scope("take1"):
+                kv_up_first(pl.ds(0, (n - 1) * CHIP))
     spread_rope()
-    with jax.named_scope("heads1a"):
-        heads(0, 0, 8)
-
-    def take_later(i, j):
-        pass_if(True, 1, j)
-        take(1, j)
-
-    @pl.when(c == 3)
-    def _():
-        with jax.named_scope("take2_wait"):
-            each_earlier_chip(take_later)
-        with jax.named_scope("heads1b"):
-            two = kv_up_second(3 * CHIP)
-            heads(0, 8, 16, lambda h: two(h - 8))
-
-    @pl.when(c < 3)
-    def _():
-        with jax.named_scope("heads1c"):
-            heads(0, 8, 16)
-        with jax.named_scope("take2_wait"):
-            each_earlier_chip(take_later)
-        for n in (1, 2):
-            @pl.when(c == n)
-            def _():
-                with jax.named_scope("take2"):
-                    two = kv_up_second(n * CHIP)
-                    for i in range(8):
-                        two(i)
-    with jax.named_scope("heads2"):
-        heads(1, 0, 16)
+    pass_if(c == 3, 1, 1)
+    with jax.named_scope("heads1"):
+        heads(0)
+
+    for n in range(NCHIP):
+        @pl.when(c == n)
+        def _():
+            if n > 0:
+                for j in ((1,), (1, 2), (3, 2))[n - 1]:
+                    pass_if(True, 1, j)
+                take(kvlat1, n * CHIP, 3)
+            with jax.named_scope("heads2"):
+                if n > 0:
+                    kv_up_second(n * CHIP)
+                heads(1)
 
     with jax.named_scope("out"):
-        wait_whole(wo_v, 9)
+        wait_whole(wo_v, 0)
         orow = pl.ds(pl.multiple_of(k * BLK, BLK), BLK)
         mine = jnp.concatenate([oall[0, orow], oall[1, orow]], axis=0)
-        acc[...] = jnp.dot(mine, wo_v[0:2048], preferred_element_type=F32)
-    with jax.named_scope("out_b"):
-        o_bytes(96, 0).wait_recv()
-        acc[...] += jnp.dot(oin[:, :1024], wo_v[2048:3072], preferred_element_type=F32)
-    with jax.named_scope("out_last"):
-        o_bytes(32, 1).wait_recv()
-        y[...] = (acc[...] + jnp.dot(oin[:, 1024:], wo_v[3072:], preferred_element_type=F32)).astype(BF16)
-
-    for item in range(2):
-        for j in (3, 2, 1):
-            @pl.when(c + j < NCHIP)
-            def _():
-                direct(item, j).wait_send()
-
-        share(item, k).wait_send()
+
+        @pl.when(k == 0)
+        def _():
+            wait_bytes(oin, 96, or_.at[0])
+            wait_bytes(oin, 32, or_.at[1])
+            y[...] = jnp.dot(jnp.concatenate([mine, oin[...]], axis=1), wo_v[...], preferred_element_type=F32).astype(BF16)
 
         @pl.when(k == 1)
         def _():
-            each_earlier_chip(lambda i, j: forward(item, j).wait_send())
-    for i in range(2):
-        q_copy(i, k).wait_send()
-    o_bytes(CHIP, 0).wait_send()
+            acc[...] = jnp.dot(mine, wo_v[0:2048], preferred_element_type=F32)
+            wait_bytes(oin, 96, or_.at[0])
+            acc[...] += jnp.dot(oin[:, :1024], wo_v[2048:3072], preferred_element_type=F32)
+            wait_bytes(oin, 32, or_.at[1])
+            y[...] = (acc[...] + jnp.dot(oin[:, 1024:], wo_v[3072:], preferred_element_type=F32)).astype(BF16)
+
+    for n in range(NCHIP):
+        @pl.when(c == n)
+        def _():
+            wait_bytes(wqd_v, 192 * (NCHIP - 1 - n) + 192 + 384, sent.at[0])
+
+            if n > 0:
+                @pl.when(k == 1)
+                def _():
+                    wait_bytes(wqd_v, 384 * n, sent.at[0])
+    wait_bytes(oin, CHIP, sent.at[1])
 
 
 def store_body(y, y1, y2, sem):
@@ -491,8 +462,7 @@
                 pltpu.VMEM((CHIP, 2048), BF16),
                 pltpu.VMEM((CHIP, D_MODEL), F32),
                 pltpu.VMEM((CHIP, KV_LAT + ROPE), F32),
-                dma((10,)), dma((2, 3)), dma((2, 3)), dma((2, 4)), dma((2, 4)),
-                dma((2,)), dma((2,)), dma((1,)), dma((2,)),
+                dma((8,)), dma((2,)), dma((2, 3)), dma((4,)), dma((1,)), dma((2,)),
             ],
             compiler_params=pltpu.CompilerParams(collective_id=0, has_side_effects=True, vmem_limit_bytes=52 * 2**20),
         )

time: 20.2 us -> 20 us (0.990)
  no operation moved by 1% of the time
where the time goes in v3:
time: 20 us; the launch traced here: 19.9 us
  Pallas kernels  19.1 us (96%)
  between operations  0.82 us (4%)
    pallas_call x1, Pallas kernels, local_body(): y = call(*(pltpu.with_memory_space_constraint(a, pltpu.HBM) for a in args))  18.3 us
    pallas_call x1, Pallas kernels, store(): pl.pallas_call(store_body, out_shape=(jax.ShapeDtypeStruct((BLK, D_MODEL)...  0.78 us

profile of v3, /device:TPU:6, one launch (start us, length us, event | category | flops | bytes accessed | tf_op | source)
XLA Modules:
  0.0 19.9 jit_solution(6761815559949548675)
XLA Ops:
  0.6 18.3 %shard_map.122.y = bf16[128,1792]{1,0:T(8,128)(2,1)S(1)} custom-call(bf16[64,1792]{1,0:T(8,128)(2,1)} %x1.1, s32[1,64]{1,0:T(1,128)} %bitcast.4, bf16[64,1792]{1,0:T(8,128)(2,1)} %x2.1, s32[1,64]{1,0:T(1,128)} %bitcast.5, bf16[1792,384]{1,0:T(8,128)(2,1)} %wqd.1, bf16[384]{0:T(512)(128)(2,1)} %gq.1, bf16[384,6144]{1,0:T(8,128)(2,1)} %wqu.1, ...), custom_call_target="tpu_custom_call" | custom-call | tf_op jit(solution)/shard_map/pallas_call | solution.py:471
  18.9 0.8 %shard_map.123 = (bf16[64,1792]{1,0:T(8,128)(2,1)}, bf16[64,1792]{1,0:T(8,128)(2,1)}) custom-call(bf16[128,1792]{1,0:T(8,128)(2,1)S(1)} %shard_map.122.y), custom_call_target="tpu_custom_call" | custom-call | tf_op jit(solution)/shard_map/pallas_call | solution.py:418

commit v4 on v3

--- a/solution.py
+++ b/solution.py
@@ -81,6 +81,7 @@
         @pl.when(c < b)
         def _():
             kvlat0[pl.ds(b * CHIP, CHIP), KV_LAT:] = jnp.zeros((CHIP, 128), BF16)
+            kvlat1[pl.ds(b * CHIP, CHIP)] = jnp.zeros((CHIP, KV_LAT), BF16)
 
             def zero(h, _):
                 for mb in range(2):
@@ -162,7 +163,7 @@
 
     def forward(item, j):
         p = kvlat[item].at[chip_rows(c - j)]
-        return pltpu.make_async_remote_copy(src_ref=p, dst_ref=p, send_sem=sent.at[0], recv_sem=fr.at[3 if item else 1 if j == 1 else 2],
+        return pltpu.make_async_remote_copy(src_ref=p, dst_ref=p, send_sem=sent.at[0], recv_sem=fr.at[2 * item + (1 if j == 1 else 2)],
                                             device_id=partner, device_id_type=MESH)
 
     def send(item, pairs):
@@ -223,11 +224,11 @@
             s = slice(mb * BLK, (mb + 1) * BLK)
             kT[mb, h, :, chip_rows(c)] = jnp.concatenate([key[s], kheld[h, s]], axis=0).T
 
-    def kv_up_first(r):
+    def kv_up_rows(mb, r):
         def store(h, key, val):
-            kT[0, h, :, r] = key
-            vb[0, h, r] = val
-        kv_up(kvlat0[r, :KV_LAT], store)
+            kT[mb, h, :, r] = key
+            vb[mb, h, r] = val
+        kv_up(kvlat[mb][r, :KV_LAT], store)
 
     send(1, ((2, 1),))
     with jax.named_scope("wait_wkvu"):
@@ -278,14 +279,15 @@
         def _():
             wait_share()
             kv_up_own()
-            queries()
 
         @pl.when(k == 1)
         def _():
             kv_up_device(k, hold_key)
             wait_share()
             kv_up_device(pk, join_key)
-            queries()
+
+    with jax.named_scope("queries"):
+        queries()
 
     def pass_on(item, j):
         direct_recv(item, j).wait_recv()
@@ -311,28 +313,30 @@
             half = r[mb * ROPE:(mb + 1) * ROPE]
             kropeT[mb] = jnp.concatenate([half, half], axis=0)
 
-    def heads(mb):
+    def heads(mb, kv_up_first, then={}):
         scores = []
+        if mb == 1:
+            kv_up_first()
         for h in range(HEADS):
             kcat = jnp.concatenate([kT[mb, h], kropeT[mb]], axis=0)
             scores.append(jnp.dot(qbuf[mb, h], kcat, preferred_element_type=F32))
+        if mb == 0:
+            kv_up_first()
         probs = []
-        for s in scores:
+        for h, s in enumerate(scores):
             s = jnp.minimum(s, bias[mb])
             m = jnp.max(s, axis=1, keepdims=True)
             e = jnp.exp2((s - m) * SCALE2)
             probs.append((e * (1.0 / jnp.sum(e, axis=1, keepdims=True))).astype(BF16))
+            if h in then:
+                then[h]()
         for h in range(HEADS):
             o = jnp.dot(probs[h], vb[mb, h], preferred_element_type=F32)
             oall[mb, :, h * 128:(h + 1) * 128] = o.astype(BF16)
-            if h % 8 == 7:
-                o_copy(mb, h // 8).start()
-
-    def kv_up_second(n):
-        def store(h, key, val):
-            kT[1, h, :, 0:n] = key
-            vb[1, h, 0:n] = val
-        kv_up(kvlat1[0:n], store)
+            if mb == 1 and h == 7:
+                o_copy(1, 0).start()
+        for half in ((0, 1), (1,))[mb]:
+            o_copy(mb, half).start()
 
     def take(ref, n, i):
         with jax.named_scope("take_wait"):
@@ -349,7 +353,7 @@
     def _():
         take(kvlat0, CHIP, 1)
         with jax.named_scope("take1"):
-            kv_up_first(chip_rows(c - 1))
+            kv_up_rows(0, chip_rows(c - 1))
 
     for n in (2, 3):
         @pl.when(c == n)
@@ -357,23 +361,46 @@
             pass_if(True, 0, 2)
             take(kvlat0, (n - 1) * CHIP, 2)
             with jax.named_scope("take1"):
-                kv_up_first(pl.ds(0, (n - 1) * CHIP))
+                kv_up_rows(0, pl.ds(0, (n - 1) * CHIP))
     spread_rope()
-    pass_if(c == 3, 1, 1)
-    with jax.named_scope("heads1"):
-        heads(0)
-
-    for n in range(NCHIP):
-        @pl.when(c == n)
-        def _():
-            if n > 0:
-                for j in ((1,), (1, 2), (3, 2))[n - 1]:
-                    pass_if(True, 1, j)
-                take(kvlat1, n * CHIP, 3)
-            with jax.named_scope("heads2"):
-                if n > 0:
-                    kv_up_second(n * CHIP)
-                heads(1)
+    @pl.when(c == 3)
+    def _():
+        pass_if(True, 1, 1)
+        take(kvlat1, CHIP, 3)
+
+    def third_rows():
+        kv_up_rows(1, pl.ds(2 * CHIP, CHIP))
+
+    late = jnp.logical_and(k == 1, c == 3)
+
+    @pl.when(late)
+    def _():
+        with jax.named_scope("heads1"):
+            heads(0, third_rows, {3: lambda: pass_on(1, 3), 8: lambda: pass_on(1, 2)})
+
+    @pl.when(jnp.logical_not(late))
+    def _():
+        with jax.named_scope("heads1"):
+            heads(0, third_rows)
+
+    @pl.when(c == 1)
+    def _():
+        pass_if(True, 1, 1)
+        take(kvlat1, CHIP, 3)
+
+    @pl.when(c == 2)
+    def _():
+        for j in (1, 2):
+            pass_if(True, 1, j)
+        for i in (3, 4):
+            take(kvlat1, CHIP, i)
+
+    @pl.when(c == 3)
+    def _():
+        take(kvlat1, 2 * CHIP, 4)
+
+    with jax.named_scope("heads2"):
+        heads(1, lambda: kv_up_rows(1, pl.ds(0, 2 * CHIP)))
 
     with jax.named_scope("out"):
         wait_whole(wo_v, 0)
@@ -462,7 +489,7 @@
                 pltpu.VMEM((CHIP, 2048), BF16),
                 pltpu.VMEM((CHIP, D_MODEL), F32),
                 pltpu.VMEM((CHIP, KV_LAT + ROPE), F32),
-                dma((8,)), dma((2,)), dma((2, 3)), dma((4,)), dma((1,)), dma((2,)),
+                dma((8,)), dma((2,)), dma((2, 3)), dma((5,)), dma((1,)), dma((2,)),
             ],
             compiler_params=pltpu.CompilerParams(collective_id=0, has_side_effects=True, vmem_limit_bytes=52 * 2**20),
         )

time: 20 us -> 19.5 us (0.975)
  Pallas kernels: 19.1 us -> 18.6 us
    pallas_call x1, Pallas kernels: 18.3 us -> 17.8 us  [local_body(): y = call(*(pltpu.with_memory_space_constraint(a, pltpu.HBM) for a in args))]
where the time goes in v4:
time: 19.5 us; the launch traced here: 19.4 us
  Pallas kernels  18.6 us (95%)
  between operations  0.8 us (4%)
    pallas_call x1, Pallas kernels, local_body(): y = call(*(pltpu.with_memory_space_constraint(a, pltpu.HBM) for a in args))  17.8 us
    pallas_call x1, Pallas kernels, store(): pl.pallas_call(store_body, out_shape=(jax.ShapeDtypeStruct((BLK, D_MODEL)...  0.78 us

profile of v4, /device:TPU:6, one launch (start us, length us, event | category | flops | bytes accessed | tf_op | source)
XLA Modules:
  0.0 19.4 jit_solution(4523128114968360160)
XLA Ops:
  0.6 17.8 %shard_map.122.y = bf16[128,1792]{1,0:T(8,128)(2,1)S(1)} custom-call(bf16[64,1792]{1,0:T(8,128)(2,1)} %x1.1, s32[1,64]{1,0:T(1,128)} %bitcast.4, bf16[64,1792]{1,0:T(8,128)(2,1)} %x2.1, s32[1,64]{1,0:T(1,128)} %bitcast.5, bf16[1792,384]{1,0:T(8,128)(2,1)} %wqd.1, bf16[384]{0:T(512)(128)(2,1)} %gq.1, bf16[384,6144]{1,0:T(8,128)(2,1)} %wqu.1, ...), custom_call_target="tpu_custom_call" | custom-call | tf_op jit(solution)/shard_map/pallas_call | solution.py:498
  18.5 0.8 %shard_map.123 = (bf16[64,1792]{1,0:T(8,128)(2,1)}, bf16[64,1792]{1,0:T(8,128)(2,1)}) custom-call(bf16[128,1792]{1,0:T(8,128)(2,1)S(1)} %shard_map.122.y), custom_call_target="tpu_custom_call" | custom-call | tf_op jit(solution)/shard_map/pallas_call | solution.py:445

commit v5 on v4

--- a/solution.py
+++ b/solution.py
@@ -21,11 +21,12 @@
 NCHIP = 4
 LN_BASE = 9.210340371976184
 EPS = 1e-6
-LEAD = 4
 K_A = 1024
 SCALE2 = 192 ** -0.5 * 1.4426950408889634
 NEG = -1e30
 BIG = 3.0e38
+OFF = -1.5e38
+OWN = 3 * CHIP
 
 
 def norm_rows(z, gain):
@@ -35,7 +36,7 @@
 
 def body(x1, p1, x2, p2, wqd, gq, wqu, wkvd, gkv, wkvu, wo, y,
          xv, posv, wqd_v, gq_v, wqu_v, wkvd_v, gkv_v, wkvu_v, wo_v,
-         kvlat0, kvlat1, qlat, tabs, qbuf, kheld, kT, vb, kropeT, bias, oall, oin, acc, usum,
+         kvlat0, kvlat1, qlat, tabs, qbuf, kheld, kT, vb, kropeT, start, flags, causal, oall, oin, acc, usum,
          lsem, sent, dr, fr, qr, or_):
     kvlat = (kvlat0, kvlat1)
     sp = lax.axis_index("sp")
@@ -77,21 +78,26 @@
         for core in range(2):
             pl.semaphore_signal(barrier, inc=1, device_id=dev(lax.rem(c + j, NCHIP), core), device_id_type=MESH)
 
-    for b in range(1, NCHIP):
+    for b in range(NCHIP - 1):
+        @pl.when(c <= b)
+        def _():
+            def zero(h, _):
+                kT[0, h, :, pl.ds(b * CHIP, CHIP)] = jnp.zeros((128, CHIP), BF16)
+                vb[0, h, pl.ds(b * CHIP, CHIP)] = jnp.zeros((CHIP, 128), BF16)
+                return 0
+            lax.fori_loop(0, HEADS, zero, 0)
+
         @pl.when(c < b)
         def _():
             kvlat0[pl.ds(b * CHIP, CHIP), KV_LAT:] = jnp.zeros((CHIP, 128), BF16)
             kvlat1[pl.ds(b * CHIP, CHIP)] = jnp.zeros((CHIP, KV_LAT), BF16)
 
-            def zero(h, _):
-                for mb in range(2):
-                    kT[mb, h, :, pl.ds(b * CHIP, CHIP)] = jnp.zeros((128, CHIP), BF16)
-                    vb[mb, h, pl.ds(b * CHIP, CHIP)] = jnp.zeros((CHIP, 128), BF16)
-                return 0
-            lax.fori_loop(0, HEADS, zero, 0)
+    tri = lax.broadcasted_iota(jnp.int32, (CHIP, CHIP), 1) <= lax.broadcasted_iota(jnp.int32, (CHIP, CHIP), 0)
+    causal[...] = jnp.where(tri, BIG, NEG)
 
     lane = lax.broadcasted_iota(jnp.int32, (1, 128), 1)
     lo64 = lane < 64
+    lane64 = lax.rem(lane, 64)
     lo32 = lax.rem(lane, 64) < 32
 
     wait_whole(posv, 0)
@@ -203,8 +209,8 @@
 
         def store(h, key, val):
             for mb in range(2):
-                kT[mb, h, :, r] = key[:, mb * CHIP:(mb + 1) * CHIP]
-                vb[mb, h, r] = val[mb * CHIP:(mb + 1) * CHIP]
+                kT[mb, h, :, OWN:] = key[:, mb * CHIP:(mb + 1) * CHIP]
+                vb[mb, h, OWN:] = val[mb * CHIP:(mb + 1) * CHIP]
         kv_up(jnp.concatenate([kvlat0[r, :KV_LAT], kvlat1[r]], axis=0), store)
 
     def kv_up_device(core, store_key):
@@ -213,7 +219,7 @@
         def store(h, key, val):
             store_key(h, key)
             for mb in range(2):
-                vb[mb, h, r] = val[mb * BLK:(mb + 1) * BLK]
+                vb[mb, h, pl.ds(pl.multiple_of(OWN + core * BLK, BLK), BLK)] = val[mb * BLK:(mb + 1) * BLK]
         kv_up(jnp.concatenate([kvlat0[r, :KV_LAT], kvlat1[r]], axis=0), store, False)
 
     def hold_key(h, key):
@@ -222,7 +228,7 @@
     def join_key(h, key):
         for mb in range(2):
             s = slice(mb * BLK, (mb + 1) * BLK)
-            kT[mb, h, :, chip_rows(c)] = jnp.concatenate([key[s], kheld[h, s]], axis=0).T
+            kT[mb, h, :, OWN:] = jnp.concatenate([key[s], kheld[h, s]], axis=0).T
 
     def kv_up_rows(mb, r):
         def store(h, key, val):
@@ -247,9 +253,8 @@
             t0, t1, t2 = (f[:, pair * 384 + n * 128: pair * 384 + (n + 1) * 128] for n in range(3))
             n1 = pltpu.roll(jnp.where(lo64, t2, t1), 64, 1)
             r = rot(jnp.where(lo64, t1, t2), tabs[0], tabs[1])
-            zero = jnp.zeros_like(r)
-            q = ((t0.astype(BF16), jnp.where(lo64, r, zero).astype(BF16)),
-                 (n1.astype(BF16), jnp.where(lo64, zero, r).astype(BF16)))
+            q = ((t0.astype(BF16), jnp.where(lo64, r, flags[...]).astype(BF16)),
+                 (n1.astype(BF16), jnp.where(lo64, flags[...], r).astype(BF16)))
             for odd in range(2):
                 h = i * 4 + pair * 2 + odd
                 for mb in range(2):
@@ -260,13 +265,22 @@
 
     def queries():
         wait_bytes(wqd_v, 384, qr.at[0])
+        row = lax.broadcasted_iota(jnp.int32, (2 * CHIP, 1), 0)
+        index = c * CHIP + lax.div(row, CHIP) * BLK + lax.rem(row, BLK)
+        start[...] = index.astype(F32) - tabs[2]
+        flags[...] = jnp.where(lane64 == 0, (start[...] > 0.5).astype(F32), (lane64 == 1).astype(F32))
+        col = lax.broadcasted_iota(jnp.int32, (ROPE, TOK), 1)
+        kind = lax.broadcasted_iota(jnp.int32, (ROPE, TOK), 0)
+        place = jnp.where(col < OWN, col, c * CHIP + col - OWN).astype(F32)
+        empty = jnp.logical_and(col >= c * CHIP, col < OWN)
         for mb in range(2):
-            for core in range(2):
-                pos = tabs[2, pl.ds(core * CHIP + mb * BLK, BLK), 0:1].astype(jnp.int32)
-                qi = c * CHIP + core * BLK + lax.broadcasted_iota(jnp.int32, (BLK, TOK), 0)
-                ki = lax.broadcasted_iota(jnp.int32, (BLK, TOK), 1)
-                keep = jnp.logical_and(ki <= qi, ki >= qi - pos)
-                bias[mb, pl.ds(core * BLK, BLK)] = jnp.where(keep, BIG, NEG)
+            firsts = [jnp.max(start[pl.ds(core * CHIP + mb * BLK, BLK)], axis=0, keepdims=True) for core in range(2)]
+            first = jnp.maximum(firsts[0], firsts[1])
+            before = place < jnp.concatenate([first] * 4, axis=1)
+            off = jnp.logical_or(jnp.logical_and(kind == 0, before), jnp.logical_and(kind == 1, empty))
+            masks = jnp.where(off, OFF, 0.0).astype(BF16)
+            kropeT[mb, 0, ROPE:] = masks
+            kropeT[mb, 1, :ROPE] = masks
         l_wqu.wait()
         prev = q_up(0)
         for i in range(4):
@@ -307,24 +321,24 @@
             src_ref=oall.at[mb, pl.ds(pl.multiple_of(pk * BLK, BLK), BLK), cs], dst_ref=oin.at[pl.ds(mb * BLK, BLK), cs],
             send_sem=sent.at[1], recv_sem=or_.at[mb * half], device_id=partner, device_id_type=MESH)
 
-    def spread_rope():
-        r = kvlat0[:, KV_LAT:].T
+    def shared_keys():
+        r = jnp.concatenate([kvlat0[0:OWN, KV_LAT:], kvlat0[chip_rows(c), KV_LAT:]], axis=0).T
         for mb in range(2):
-            half = r[mb * ROPE:(mb + 1) * ROPE]
-            kropeT[mb] = jnp.concatenate([half, half], axis=0)
+            kropeT[mb, 0, :ROPE] = r[mb * ROPE:(mb + 1) * ROPE]
+            kropeT[mb, 1, ROPE:] = r[mb * ROPE:(mb + 1) * ROPE]
 
     def heads(mb, kv_up_first, then={}):
         scores = []
         if mb == 1:
             kv_up_first()
         for h in range(HEADS):
-            kcat = jnp.concatenate([kT[mb, h], kropeT[mb]], axis=0)
+            kcat = jnp.concatenate([kT[mb, h], kropeT[mb, h % 2]], axis=0)
             scores.append(jnp.dot(qbuf[mb, h], kcat, preferred_element_type=F32))
         if mb == 0:
             kv_up_first()
         probs = []
         for h, s in enumerate(scores):
-            s = jnp.minimum(s, bias[mb])
+            s = jnp.concatenate([s[:, :OWN], jnp.minimum(s[:, OWN:], causal[...])], axis=1)
             m = jnp.max(s, axis=1, keepdims=True)
             e = jnp.exp2((s - m) * SCALE2)
             probs.append((e * (1.0 / jnp.sum(e, axis=1, keepdims=True))).astype(BF16))
@@ -362,7 +376,7 @@
             take(kvlat0, (n - 1) * CHIP, 2)
             with jax.named_scope("take1"):
                 kv_up_rows(0, pl.ds(0, (n - 1) * CHIP))
-    spread_rope()
+    shared_keys()
     @pl.when(c == 3)
     def _():
         pass_if(True, 1, 1)
@@ -483,8 +497,10 @@
                 pltpu.VMEM((HEADS, CHIP, 128), BF16),
                 pltpu.VMEM((2, HEADS, 128, TOK), BF16),
                 pltpu.VMEM((2, HEADS, TOK, 128), BF16),
-                pltpu.VMEM((2, 128, TOK), BF16),
-                pltpu.VMEM((2, CHIP, TOK), F32),
+                pltpu.VMEM((2, 2, 128, TOK), BF16),
+                pltpu.VMEM((2 * CHIP, 128), F32),
+                pltpu.VMEM((2 * CHIP, 128), F32),
+                pltpu.VMEM((CHIP, CHIP), F32),
                 pltpu.VMEM((2, CHIP, 2048), BF16),
                 pltpu.VMEM((CHIP, 2048), BF16),
                 pltpu.VMEM((CHIP, D_MODEL), F32),

time: 19.5 us -> 19.2 us (0.985)
  Pallas kernels: 18.6 us -> 18.3 us
    pallas_call x1, Pallas kernels: 17.8 us -> 17.5 us  [local_body(): y = call(*(pltpu.with_memory_space_constraint(a, pltpu.HBM) for a in args))]
where the time goes in v5:
time: 19.2 us; the launch traced here: 19.1 us
  Pallas kernels  18.3 us (95%)
  between operations  0.8 us (4%)
    pallas_call x1, Pallas kernels, local_body(): y = call(*(pltpu.with_memory_space_constraint(a, pltpu.HBM) for a in args))  17.5 us
    pallas_call x1, Pallas kernels, store(): pl.pallas_call(store_body, out_shape=(jax.ShapeDtypeStruct((BLK, D_MODEL)...  0.78 us

profile of v5, /device:TPU:6, one launch (start us, length us, event | category | flops | bytes accessed | tf_op | source)
XLA Modules:
  0.0 19.1 jit_solution(4390712829116264794)
XLA Ops:
  0.6 17.5 %shard_map.122.y = bf16[128,1792]{1,0:T(8,128)(2,1)S(1)} custom-call(bf16[64,1792]{1,0:T(8,128)(2,1)} %x1.1, s32[1,64]{1,0:T(1,128)} %bitcast.4, bf16[64,1792]{1,0:T(8,128)(2,1)} %x2.1, s32[1,64]{1,0:T(1,128)} %bitcast.5, bf16[1792,384]{1,0:T(8,128)(2,1)} %wqd.1, bf16[384]{0:T(512)(128)(2,1)} %gq.1, bf16[384,6144]{1,0:T(8,128)(2,1)} %wqu.1, ...), custom_call_target="tpu_custom_call" | custom-call | tf_op jit(solution)/shard_map/pallas_call | solution.py:514
  18.2 0.8 %shard_map.123 = (bf16[64,1792]{1,0:T(8,128)(2,1)}, bf16[64,1792]{1,0:T(8,128)(2,1)}) custom-call(bf16[128,1792]{1,0:T(8,128)(2,1)S(1)} %shard_map.122.y), custom_call_target="tpu_custom_call" | custom-call | tf_op jit(solution)/shard_map/pallas_call | solution.py:459

commit v6 on v5

--- a/solution.py
+++ b/solution.py
@@ -21,7 +21,7 @@
 NCHIP = 4
 LN_BASE = 9.210340371976184
 EPS = 1e-6
-K_A = 1024
+K_A = 768
 SCALE2 = 192 ** -0.5 * 1.4426950408889634
 NEG = -1e30
 BIG = 3.0e38
@@ -197,12 +197,16 @@
     for i in range(2):
         q_copy(i, k).start()
 
+    def turned(h, key):
+        t = key.T
+        return jnp.concatenate([t[64:], t[:64]], axis=0) if h % 2 else t
+
     def kv_up(lhs, store, turn=True):
         for i in range(4):
             kv = jnp.dot(lhs, wkvu_v[:, i * 1024:(i + 1) * 1024], preferred_element_type=F32).astype(BF16)
             for n in range(4):
                 key = kv[:, n * 256:n * 256 + NOPE]
-                store(i * 4 + n, key.T if turn else key, kv[:, n * 256 + NOPE:(n + 1) * 256])
+                store(i * 4 + n, turned(i * 4 + n, key) if turn else key, kv[:, n * 256 + NOPE:(n + 1) * 256])
 
     def kv_up_own():
         r = chip_rows(c)
@@ -228,7 +232,7 @@
     def join_key(h, key):
         for mb in range(2):
             s = slice(mb * BLK, (mb + 1) * BLK)
-            kT[mb, h, :, OWN:] = jnp.concatenate([key[s], kheld[h, s]], axis=0).T
+            kT[mb, h, :, OWN:] = turned(h, jnp.concatenate([key[s], kheld[h, s]], axis=0))
 
     def kv_up_rows(mb, r):
         def store(h, key, val):
@@ -251,7 +255,7 @@
     def q_store(i, f):
         for pair in range(2):
             t0, t1, t2 = (f[:, pair * 384 + n * 128: pair * 384 + (n + 1) * 128] for n in range(3))
-            n1 = pltpu.roll(jnp.where(lo64, t2, t1), 64, 1)
+            n1 = jnp.where(lo64, t2, t1)
             r = rot(jnp.where(lo64, t1, t2), tabs[0], tabs[1])
             q = ((t0.astype(BF16), jnp.where(lo64, r, flags[...]).astype(BF16)),
                  (n1.astype(BF16), jnp.where(lo64, flags[...], r).astype(BF16)))

time: 19.2 us -> 19.2 us (level)
  no operation moved by 1% of the time
where the time goes in v6:
time: 19.2 us; the launch traced here: 19.1 us
  Pallas kernels  18.3 us (95%)
  between operations  0.8 us (4%)
    pallas_call x1, Pallas kernels, local_body(): y = call(*(pltpu.with_memory_space_constraint(a, pltpu.HBM) for a in args))  17.5 us
    pallas_call x1, Pallas kernels, store(): pl.pallas_call(store_body, out_shape=(jax.ShapeDtypeStruct((BLK, D_MODEL)...  0.78 us

profile of v6, /device:TPU:6, one launch (start us, length us, event | category | flops | bytes accessed | tf_op | source)
XLA Modules:
  0.0 19.1 jit_solution(2667250202577539466)
XLA Ops:
  0.6 17.5 %shard_map.122.y = bf16[128,1792]{1,0:T(8,128)(2,1)S(1)} custom-call(bf16[64,1792]{1,0:T(8,128)(2,1)} %x1.1, s32[1,64]{1,0:T(1,128)} %bitcast.4, bf16[64,1792]{1,0:T(8,128)(2,1)} %x2.1, s32[1,64]{1,0:T(1,128)} %bitcast.5, bf16[1792,384]{1,0:T(8,128)(2,1)} %wqd.1, bf16[384]{0:T(512)(128)(2,1)} %gq.1, bf16[384,6144]{1,0:T(8,128)(2,1)} %wqu.1, ...), custom_call_target="tpu_custom_call" | custom-call | tf_op jit(solution)/shard_map/pallas_call | solution.py:518
  18.1 0.8 %shard_map.123 = (bf16[64,1792]{1,0:T(8,128)(2,1)}, bf16[64,1792]{1,0:T(8,128)(2,1)}) custom-call(bf16[128,1792]{1,0:T(8,128)(2,1)S(1)} %shard_map.122.y), custom_call_target="tpu_custom_call" | custom-call | tf_op jit(solution)/shard_map/pallas_call | solution.py:463

commit v7 on v6

--- a/solution.py
+++ b/solution.py
@@ -394,7 +394,7 @@
     @pl.when(late)
     def _():
         with jax.named_scope("heads1"):
-            heads(0, third_rows, {3: lambda: pass_on(1, 3), 8: lambda: pass_on(1, 2)})
+            heads(0, third_rows, {5: lambda: pass_on(1, 3), 9: lambda: pass_on(1, 2)})
 
     @pl.when(jnp.logical_not(late))
     def _():

time: 19.2 us -> 19.2 us (level)
  no operation moved by 1% of the time
where the time goes in v7:
time: 19.2 us; the launch traced here: 19 us
  Pallas kernels  18.2 us (95%)
  between operations  0.8 us (4%)
    pallas_call x1, Pallas kernels, local_body(): y = call(*(pltpu.with_memory_space_constraint(a, pltpu.HBM) for a in args))  17.4 us
    pallas_call x1, Pallas kernels, store(): pl.pallas_call(store_body, out_shape=(jax.ShapeDtypeStruct((BLK, D_MODEL)...  0.78 us

profile of v7, /device:TPU:6, one launch (start us, length us, event | category | flops | bytes accessed | tf_op | source)
XLA Modules:
  0.0 19.0 jit_solution(10728552107772532130)
XLA Ops:
  0.6 17.4 %shard_map.122.y = bf16[128,1792]{1,0:T(8,128)(2,1)S(1)} custom-call(bf16[64,1792]{1,0:T(8,128)(2,1)} %x1.1, s32[1,64]{1,0:T(1,128)} %bitcast.4, bf16[64,1792]{1,0:T(8,128)(2,1)} %x2.1, s32[1,64]{1,0:T(1,128)} %bitcast.5, bf16[1792,384]{1,0:T(8,128)(2,1)} %wqd.1, bf16[384]{0:T(512)(128)(2,1)} %gq.1, bf16[384,6144]{1,0:T(8,128)(2,1)} %wqu.1, ...), custom_call_target="tpu_custom_call" | custom-call | tf_op jit(solution)/shard_map/pallas_call | solution.py:518
  18.1 0.8 %shard_map.123 = (bf16[64,1792]{1,0:T(8,128)(2,1)}, bf16[64,1792]{1,0:T(8,128)(2,1)}) custom-call(bf16[128,1792]{1,0:T(8,128)(2,1)S(1)} %shard_map.122.y), custom_call_target="tpu_custom_call" | custom-call | tf_op jit(solution)/shard_map/pallas_call | solution.py:463

commit v8 on v7

--- a/solution.py
+++ b/solution.py
@@ -394,7 +394,7 @@
     @pl.when(late)
     def _():
         with jax.named_scope("heads1"):
-            heads(0, third_rows, {5: lambda: pass_on(1, 3), 9: lambda: pass_on(1, 2)})
+            heads(0, third_rows, {6: lambda: pass_on(1, 3), 10: lambda: pass_on(1, 2)})
 
     @pl.when(jnp.logical_not(late))
     def _():

time: 19.2 us -> 19.2 us (level)
  no operation moved by 1% of the time
where the time goes in v8:
time: 19.2 us; the launch traced here: 19 us
  Pallas kernels  18.2 us (95%)
  between operations  0.8 us (4%)
    pallas_call x1, Pallas kernels, local_body(): y = call(*(pltpu.with_memory_space_constraint(a, pltpu.HBM) for a in args))  17.4 us
    pallas_call x1, Pallas kernels, store(): pl.pallas_call(store_body, out_shape=(jax.ShapeDtypeStruct((BLK, D_MODEL)...  0.78 us

profile of v8, /device:TPU:6, one launch (start us, length us, event | category | flops | bytes accessed | tf_op | source)
XLA Modules:
  0.0 19.0 jit_solution(5573598568314465134)
XLA Ops:
  0.6 17.4 %shard_map.122.y = bf16[128,1792]{1,0:T(8,128)(2,1)S(1)} custom-call(bf16[64,1792]{1,0:T(8,128)(2,1)} %x1.1, s32[1,64]{1,0:T(1,128)} %bitcast.4, bf16[64,1792]{1,0:T(8,128)(2,1)} %x2.1, s32[1,64]{1,0:T(1,128)} %bitcast.5, bf16[1792,384]{1,0:T(8,128)(2,1)} %wqd.1, bf16[384]{0:T(512)(128)(2,1)} %gq.1, bf16[384,6144]{1,0:T(8,128)(2,1)} %wqu.1, ...), custom_call_target="tpu_custom_call" | custom-call | tf_op jit(solution)/shard_map/pallas_call | solution.py:518
  18.1 0.8 %shard_map.123 = (bf16[64,1792]{1,0:T(8,128)(2,1)}, bf16[64,1792]{1,0:T(8,128)(2,1)}) custom-call(bf16[128,1792]{1,0:T(8,128)(2,1)S(1)} %shard_map.122.y), custom_call_target="tpu_custom_call" | custom-call | tf_op jit(solution)/shard_map/pallas_call | solution.py:463
